TPU v7x, 256 devices: a whole 4x4x8 slice. The times are simulated.
256 devices in a mesh: section: 8 (over z_hi, core), expert: 32 (over z_lo, x, y).
Axes of the slice: x: 4, y: 4, z: 8 (z_hi: 4, z_lo: 2; z = z_hi * 2 + z_lo), core: 2. Of those that a mesh axis runs over, the one named last changes fastest.
Arguments:
- act_in: bfloat16 [8, 4096, 7168], P('section', 'expert'), may hold values from -6 to 6
- cotangent: bfloat16 [8, 4096, 7168], P('section', 'expert'), may hold values from -6 to 6
- fwd_ids: int32 [8, 4096, 8], P('section', 'expert'), may hold values from 0 to 255, as said below
- fwd_gates: float32 [8, 4096, 8], P('section', 'expert'), may hold values from 0.05 to 0.8
- bwd_ids: int32 [8, 4096, 8], P('section', 'expert'), may hold values from 0 to 255, as said below
- bwd_gates: float32 [8, 4096, 8], P('section', 'expert'), may hold values from 0.05 to 0.8
- gate_w: bfloat16 [8, 7168, 4096], P('section', None, 'expert'), may hold values from -0.0625 to 0.0625
- up_w: bfloat16 [8, 7168, 4096], P('section', None, 'expert'), may hold values from -0.0625 to 0.0625
- down_w: bfloat16 [8, 4096, 7168], P('section', 'expert'), may hold values from -0.125 to 0.125
- gate_pre: bfloat16 [8, 320, 4096], P('section', None, 'expert'), may hold values from -6 to 6
- up_pre: bfloat16 [8, 320, 4096], P('section', None, 'expert'), may hold values from -6 to 6
Outputs:
- next_act: bfloat16 [8, 4096, 7168], P('section', 'expert')
- prev_grad: bfloat16 [8, 4096, 7168], P('section', 'expert')
- gate_grad: float32 [8, 4096, 8], P('section', 'expert')
Inputs may be any that keep to these rules, and one draw needn't show every extreme that they name: `fwd_ids`: the 8 ids of a row differ. In each aligned block of 128 rows (the rows of one device) each id below 2 is named by at most 10 rows; in every section one such id is named by exactly 10 rows in every block. `bwd_ids`: as for fwd_ids.
All inputs are finite; a program needn't handle non-finite values.
Results may differ from a plain program's by a relative error of at most 0.012.
Values may be sent and summed in bfloat16 or wider, within the bound.
A program may use at most 128 MiB of HBM per device.

v0:
```python
import math

import jax
import jax.numpy as jnp
from jax import lax
from jax.sharding import PartitionSpec as P

FF = 2048


def in_blocks(shard, dim, devices):
    before, after = (shard.shape[:dim], shard.shape[dim + 1 :])
    return jnp.moveaxis(shard.reshape(*before, devices, -1, *after), dim, 0)


def edges_of(length, count):
    turn = length // count
    if turn >= 8:
        turn -= turn % 8
    return [turn * k for k in range(1, count)]


def joined_along(pieces, dim):
    pieces = jnp.moveaxis(pieces, 0, dim)
    shape = pieces.shape
    return pieces.reshape(*shape[:dim], shape[dim] * shape[dim + 1], *shape[dim + 2 :])


def cut_exchange(shard, axis, pieces, split_dim, concat_dim):
    blocks = in_blocks(shard, split_dim, lax.axis_size(axis))
    cut = max(range(1, max(2, blocks.ndim - 1)), key=lambda d: blocks.shape[d])
    gathered = []
    for section in jnp.split(blocks, edges_of(blocks.shape[cut], pieces), axis=cut):
        if section.size:
            gathered.append(lax.all_to_all(section, axis, split_axis=0, concat_axis=0, tiled=True))
    return joined_along(jnp.concatenate(gathered, axis=cut), concat_dim)


def side_by_side(arrays, axis, split_dim, concat_dim, along):
    widths = [math.prod(a.shape[along:]) for a in arrays]
    both = jnp.concatenate(
        [a.reshape(*a.shape[:along], w) for a, w in zip(arrays, widths)], axis=along
    )
    result = lax.all_to_all(both, axis, split_axis=split_dim, concat_axis=concat_dim, tiled=True)
    pieces = jnp.split(result, [sum(widths[:k]) for k in range(1, len(widths))], axis=along)
    return tuple(
        (b.reshape(*result.shape[:along], *a.shape[along:]) for a, b in zip(arrays, pieces))
    )


def from_behind(value, axis, steps):
    count = lax.axis_size(axis)
    pairs = [(source, (source + steps) % count) for source in range(count)]
    return lax.ppermute(value, axis, pairs)


def routing(ids, gates, experts, capacity):
    expert_ids = jnp.arange(experts, dtype=jnp.int32)
    matches = ids[None, :, :] == expert_ids[:, None, None]
    routed = jnp.any(matches, axis=2)
    weights = jnp.sum(jnp.where(matches, gates[None, :, :], 0.0), axis=2)
    position = jnp.cumsum(routed.astype(jnp.int32), axis=1) - 1
    slot_ids = jnp.arange(capacity, dtype=jnp.int32)
    placing = (position[:, None, :] == slot_ids[None, :, None]) & routed[:, None, :]
    return (matches, placing.astype(jnp.float32), weights)


def send_rows(tokens, placing):
    buffer = jnp.einsum(
        "ect,td->ecd", placing.astype(jnp.bfloat16), tokens, preferred_element_type=jnp.float32
    ).astype(jnp.bfloat16)
    experts, capacity, width = buffer.shape
    ndev = lax.axis_size("expert")
    slices = ndev // experts
    received = lax.all_to_all(
        jnp.repeat(buffer, slices, axis=0), "expert", split_axis=0, concat_axis=0, tiled=True
    )
    return received.reshape(ndev * capacity, width)


def return_sums(partial_value, experts, capacity):
    ndev = lax.axis_size("expert")
    slices = ndev // experts
    width = partial_value.shape[1]
    rounded = partial_value.astype(jnp.bfloat16)
    back = cut_exchange(rounded.reshape(ndev, capacity, width), "expert", 2, 0, 0)
    return jnp.sum(back.reshape(experts, slices, capacity, width).astype(jnp.float32), axis=1)


def return_grads(partial_value, dots, experts, capacity):
    ndev = lax.axis_size("expert")
    slices = ndev // experts
    width = partial_value.shape[1]
    rounded = partial_value.astype(jnp.bfloat16)
    dots_rounded = dots.astype(jnp.bfloat16)
    back, back_dots = side_by_side(
        (rounded.reshape(ndev, capacity, width), dots_rounded.reshape(ndev, capacity)),
        "expert",
        0,
        0,
        2,
    )
    expert_grad = jnp.sum(
        back.reshape(experts, slices, capacity, width).astype(jnp.float32), axis=1
    )
    expert_dots = jnp.sum(back_dots.reshape(experts, slices, capacity).astype(jnp.float32), axis=1)
    return (expert_grad, expert_dots)


def body(
    act_in,
    cotangent,
    fwd_ids,
    fwd_gates,
    bwd_ids,
    bwd_gates,
    gate_w,
    up_w,
    down_w,
    gate_pre,
    up_pre,
):
    ndev = lax.axis_size("expert")
    w_gate = gate_w[0]
    w_up = up_w[0]
    w_down = down_w[0]
    ff_dev = w_gate.shape[1]
    slices = FF // ff_dev
    experts = ndev // slices
    capacity = gate_pre.shape[1] // ndev
    matches_f, placing_f, weights_f = routing(fwd_ids[0], fwd_gates[0], experts, capacity)
    slot_rows = send_rows(act_in[0], placing_f)
    gate_act = jnp.dot(slot_rows, w_gate, preferred_element_type=jnp.float32)
    up_act = jnp.dot(slot_rows, w_up, preferred_element_type=jnp.float32)
    hidden = (jax.nn.silu(gate_act) * up_act).astype(jnp.bfloat16)
    expert_out = return_sums(
        jnp.dot(hidden, w_down, preferred_element_type=jnp.float32), experts, capacity
    )
    mixed = jnp.einsum(
        "ect,ecd->td",
        placing_f * weights_f[:, None, :],
        expert_out,
        precision=lax.Precision.HIGHEST,
    )
    matches_b, placing_b, weights_b = routing(bwd_ids[0], bwd_gates[0], experts, capacity)
    grad_rows = send_rows(cotangent[0], placing_b)
    saved_gate = gate_pre[0].astype(jnp.float32)
    saved_up = up_pre[0].astype(jnp.float32)
    grad_hidden = jnp.einsum("rd,fd->rf", grad_rows, w_down, preferred_element_type=jnp.float32)
    sigmoid_gate = jax.nn.sigmoid(saved_gate)
    activated = saved_gate * sigmoid_gate
    gate_dots = jnp.sum(grad_hidden * activated * saved_up, axis=1)
    grad_gate_act = (
        grad_hidden * saved_up * sigmoid_gate * (1.0 + saved_gate * (1.0 - sigmoid_gate))
    ).astype(jnp.bfloat16)
    grad_up_act = (grad_hidden * activated).astype(jnp.bfloat16)
    grad_partial = jnp.einsum(
        "rf,df->rd", grad_gate_act, w_gate, preferred_element_type=jnp.float32
    )
    grad_partial = grad_partial + jnp.einsum(
        "rf,df->rd", grad_up_act, w_up, preferred_element_type=jnp.float32
    )
    expert_grad, expert_dots = return_grads(grad_partial, gate_dots, experts, capacity)
    input_grad = jnp.einsum(
        "ect,ecd->td",
        placing_b * weights_b[:, None, :],
        expert_grad,
        precision=lax.Precision.HIGHEST,
    )
    token_dots = jnp.einsum("ect,ec->et", placing_b, expert_dots, precision=lax.Precision.HIGHEST)
    gate_grad = jnp.sum(jnp.where(matches_b, token_dots[:, :, None], 0.0), axis=0)
    next_act = from_behind(mixed.astype(jnp.bfloat16)[None], "section", 1)
    prev_grad = from_behind(input_grad.astype(jnp.bfloat16)[None], "section", -1)
    return (next_act, prev_grad, gate_grad[None])


def solution(mesh):
    in_specs = (
        P("section", "expert", None),
        P("section", "expert", None),
        P("section", "expert", None),
        P("section", "expert", None),
        P("section", "expert", None),
        P("section", "expert", None),
        P("section", None, "expert"),
        P("section", None, "expert"),
        P("section", "expert", None),
        P("section", None, "expert"),
        P("section", None, "expert"),
    )
    out_specs = (
        P("section", "expert", None),
        P("section", "expert", None),
        P("section", "expert", None),
    )
    return jax.shard_map(body, mesh=mesh, in_specs=in_specs, out_specs=out_specs, check_vma=False)
```

profile of v0, /device:TPU:1, one launch (start us, length us, event | category | flops | bytes accessed | tf_op | source)
XLA Modules:
  0.0 520.6 jit_solution(15371524996227572271)
XLA Ops:
  0.6 0.0 copy-start
  0.6 0.8 fusion.64
  1.5 0.3 reduce_window_sum.17
  1.8 1.9 convolution_convert_fusion.2
  3.7 3.9 broadcast_in_dim.61
  7.5 0.0 copy-start.4
  7.5 9.5 %all-to-all-start = ((bf16[32,10,7168]{2,1,0:T(8,128)(2,1)}), bf16[32,10,7168]{2,1,0:T(8,128)(2,1)}, u32[]{:S(2)}, u32[]{:S(2)}) async-start(bf16[32,10,7168]{2,1,0:T(8,128)(2,1)} %bitcast.95), calls=%async_computation | async-start | bytes 14680064 | tf_op jit(solution)/shard_map/all_to_all | solution.py:75
  17.0 0.0 copy-done.4
  17.1 0.3 reduce_window_sum.18
  17.4 1.9 convolution_convert_fusion.1
  19.2 101.9 %all-to-all-done = bf16[32,10,7168]{2,1,0:T(8,128)(2,1)} async-done(((bf16[32,10,7168]{2,1,0:T(8,128)(2,1)}), bf16[32,10,7168]{2,1,0:T(8,128)(2,1)}, u32[]{:S(2)}, u32[]{:S(2)}) %all-to-all-start) | async-done | bytes 4587552 | tf_op jit(solution)/shard_map/all_to_all | solution.py:75
  121.1 3.9 broadcast_in_dim.65
  125.0 7.4 %all-to-all-start.3 = ((bf16[32,10,7168]{2,1,0:T(8,128)(2,1)}), bf16[32,10,7168]{2,1,0:T(8,128)(2,1)}, u32[]{:S(2)}, u32[]{:S(2)}) async-start(bf16[32,10,7168]{2,1,0:T(8,128)(2,1)} %bitcast.94), calls=%async_computation.3 | async-start | bytes 14680064 | tf_op jit(solution)/shard_map/all_to_all | solution.py:75
  132.4 8.0 %reshape.67 = bf16[320,7168]{1,0:T(8,128)(2,1)} reshape(bf16[32,10,7168]{2,1,0:T(8,128)(2,1)} %all-to-all-done) | data formatting | bytes 9175040 | tf_op jit(solution)/shard_map/reshape | solution.py:78
  140.5 4.2 fusion.14
  144.7 0.0 copy-done
  144.7 10.0 %convolution_convert_fusion = bf16[320,7168]{1,0:T(8,128)(2,1)} fusion(bf16[1,128,7168]{2,1,0:T(8,128)(2,1)} %param.19, bf16[320,7168]{1,0:T(8,128)(2,1)} %reshape.67, bf16[1,7168,128]{2,1,0:T(8,128)(2,1)S(1)} %copy-done, f32[320,128]{1,0:T(8,128)S(1)} %fusion.14), kind=kOutput, calls=%fused_computation.3 | convolution fusion | flops 1176944640 | bytes 13008896 | tf_op jit(solution)/shard_map/dot_general | solution.py:137
  154.7 7.8 %reshape_reshape.2 = bf16[32,1,10,7168]{3,2,0,1:T(8,128)(2,1)} reshape(bf16[320,7168]{1,0:T(8,128)(2,1)} %convolution_convert_fusion) | data formatting | bytes 9175040 | tf_op jit(solution)/shard_map/reshape;reshape | solution.py:13
  162.5 6.7 %slice_bitcast_fusion.1 = (bf16[32,1,5,7168]{3,2,1,0:T(8,128)(2,1)}, bf16[32,1,5,7168]{3,2,1,0:T(8,128)(2,1)}) fusion(bf16[32,1,10,7168]{3,2,0,1:T(8,128)(2,1)} %reshape_reshape.2), kind=kLoop, calls=%fused_computation.16 | loop fusion | bytes 9175040 | tf_op jit(solution)/shard_map/split | solution.py:33
  169.2 55.6 %all-to-all-done.3 = bf16[32,10,7168]{2,1,0:T(8,128)(2,1)} async-done(((bf16[32,10,7168]{2,1,0:T(8,128)(2,1)}), bf16[32,10,7168]{2,1,0:T(8,128)(2,1)}, u32[]{:S(2)}, u32[]{:S(2)}) %all-to-all-start.3) | async-done | bytes 4587552 | tf_op jit(solution)/shard_map/all_to_all | solution.py:75
  224.8 55.1 %all_to_all.25 = bf16[32,1,5,7168]{3,2,1,0:T(8,128)(2,1)} all-to-all(bf16[32,1,5,7168]{3,2,1,0:T(8,128)(2,1)} %get-tuple-element.5), channel_id=1, replica_groups=mesh['section'=8,'expert'=32] {'expert'}, dimensions={0} | all-to-all | bytes 4587520 | tf_op jit(solution)/shard_map/all_to_all | solution.py:35
  279.9 5.9 %all-to-all-start.2 = ((bf16[32,1,5,7168]{3,2,1,0:T(8,128)(2,1)}), bf16[32,1,5,7168]{3,2,1,0:T(8,128)(2,1)}, u32[]{:S(2)}, u32[]{:S(2)}) async-start(bf16[32,1,5,7168]{3,2,1,0:T(8,128)(2,1)} %get-tuple-element.6), calls=%async_computation.2 | async-start | bytes 7340032 | tf_op jit(solution)/shard_map/all_to_all | solution.py:35
  285.8 0.0 copy-start.2
  285.8 0.0 copy-start.3
  285.8 8.1 %reshape.69 = bf16[320,7168]{1,0:T(8,128)(2,1)} reshape(bf16[32,10,7168]{2,1,0:T(8,128)(2,1)} %all-to-all-done.3) | data formatting | bytes 9175040 | tf_op jit(solution)/shard_map/reshape | solution.py:78
  294.0 0.0 copy-done.2
  294.0 0.0 copy-done.3
  294.0 0.0 copy-start.1
  294.0 4.5 fusion.29
  298.4 0.0 copy-done.1
  298.4 1.4 fusion.12
  299.8 3.4 fusion
  303.2 7.8 %reshape.70 = bf16[32,10,7168]{2,1,0:T(8,128)(2,1)} reshape(bf16[320,7168]{1,0:T(8,128)(2,1)} %fusion) | data formatting | bytes 9175040 | tf_op jit(solution)/shard_map/reshape | solution.py:97
  311.0 0.2 convert_element_type.136
  311.3 6.8 %pad_maximum_fusion = bf16[32,10,7169]{2,1,0:T(8,128)(2,1)} fusion(bf16[32,10,1]{2,1,0:T(8,128)(2,1)S(1)} %convert_element_type.136, bf16[32,10,7168]{2,1,0:T(8,128)(2,1)} %reshape.70), kind=kLoop, calls=%fused_computation.13 | loop fusion | flops 9176320 | bytes 9176320 | tf_op jit(solution)/shard_map/concatenate | solution.py:41
  318.1 0.0 copy-start.5
  318.1 0.0 copy-start.7
  318.1 12.1 %all-to-all-done.2 = bf16[32,1,5,7168]{3,2,1,0:T(8,128)(2,1)} async-done(((bf16[32,1,5,7168]{3,2,1,0:T(8,128)(2,1)}), bf16[32,1,5,7168]{3,2,1,0:T(8,128)(2,1)}, u32[]{:S(2)}, u32[]{:S(2)}) %all-to-all-start.2) | async-done | bytes 2293792 | tf_op jit(solution)/shard_map/all_to_all | solution.py:35
  330.2 8.8 %all-to-all-start.4 = ((bf16[32,10,7169]{2,1,0:T(8,128)(2,1)}), bf16[32,10,7169]{2,1,0:T(8,128)(2,1)}, u32[]{:S(2)}, u32[]{:S(2)}) async-start(bf16[32,10,7169]{2,1,0:T(8,128)(2,1)} %pad_maximum_fusion), calls=%async_computation.4 | async-start | bytes 14942208 | tf_op jit(solution)/shard_map/all_to_all | solution.py:44
  339.0 0.0 copy-done.5
  339.0 0.0 copy-done.7
  339.1 5.6 %pad_maximum_fusion.1 = bf16[32,1,10,7168]{3,2,1,0:T(8,128)(2,1)S(1)} fusion(bf16[32,1,5,7168]{3,2,1,0:T(8,128)(2,1)} %all-to-all-done.2, bf16[32,1,5,7168]{3,2,1,0:T(8,128)(2,1)} %all_to_all.25), kind=kLoop, calls=%fused_computation.14 | loop fusion | flops 9175040 | bytes 9175040 | tf_op jit(solution)/shard_map/concatenate | solution.py:36
  344.7 1.4 convert_reduce_fusion
  346.1 4.2 fusion.4
  350.3 4.5 collective-permute-start
  354.9 102.7 %all-to-all-done.4 = bf16[32,10,7169]{2,1,0:T(8,128)(2,1)} async-done(((bf16[32,10,7169]{2,1,0:T(8,128)(2,1)}), bf16[32,10,7169]{2,1,0:T(8,128)(2,1)}, u32[]{:S(2)}, u32[]{:S(2)}) %all-to-all-start.4) | async-done | bytes 4588192 | tf_op jit(solution)/shard_map/all_to_all | solution.py:44
  457.6 0.9 split.19
  458.5 0.2 copy.62
  458.7 0.1 reshape.75
  458.8 0.1 reduce_sum.68
  458.9 0.1 copy.59
  459.0 0.1 fusion.51
  459.1 3.8 split.18
  462.9 0.0 copy-start.6
  463.0 4.2 convert_reduce_fusion.1
  467.1 0.0 copy-done.6
  467.1 0.6 select_reduce_fusion
  467.7 3.1 fusion.3
  470.8 3.9 collective-permute-start.1
  474.8 4.2 collective-permute-done
  479.0 37.5 %collective-permute-done.1 = bf16[1,128,7168]{2,1,0:T(8,128)(2,1)S(1)} collective-permute-done((bf16[1,128,7168]{2,1,0:T(8,128)(2,1)S(1)}, bf16[1,128,7168]{2,1,0:T(8,128)(2,1)S(1)}, u32[]{:S(2)}, u32[]{:S(2)}) %collective-permute-start.1) | collective-permute-done | bytes 1835040 | tf_op jit(solution)/shard_map/ppermute | solution.py:54
  516.5 2.8 copy.68
  519.4 1.2 copy.69
  (7 shorter events, 0.1 us)
Async XLA Ops:
  0.6 144.1 %copy-start = (bf16[1,7168,128]{2,1,0:T(8,128)(2,1)S(1)}, bf16[1,7168,128]{2,1,0:T(8,128)(2,1)}, u32[]{:S(2)}) copy-start(bf16[1,7168,128]{2,1,0:T(8,128)(2,1)} %param.18) | copy-start | bytes 5505028
  7.5 9.5 %copy-start.4 = (s32[1,128,8]{1,2,0:T(8,128)S(1)}, s32[1,128,8]{1,2,0:T(8,128)}, u32[]{:S(2)}) copy-start(s32[1,128,8]{1,2,0:T(8,128)} %param.15) | copy-start | bytes 12292
  7.5 113.6 %all-to-all-start = ((bf16[32,10,7168]{2,1,0:T(8,128)(2,1)}), bf16[32,10,7168]{2,1,0:T(8,128)(2,1)}, u32[]{:S(2)}, u32[]{:S(2)}) async-start(bf16[32,10,7168]{2,1,0:T(8,128)(2,1)} %bitcast.95), calls=%async_computation | async-start | bytes 14680064 | tf_op jit(solution)/shard_map/all_to_all | solution.py:75
  125.0 99.8 %all-to-all-start.3 = ((bf16[32,10,7168]{2,1,0:T(8,128)(2,1)}), bf16[32,10,7168]{2,1,0:T(8,128)(2,1)}, u32[]{:S(2)}, u32[]{:S(2)}) async-start(bf16[32,10,7168]{2,1,0:T(8,128)(2,1)} %bitcast.94), calls=%async_computation.3 | async-start | bytes 14680064 | tf_op jit(solution)/shard_map/all_to_all | solution.py:75
  279.9 50.3 %all-to-all-start.2 = ((bf16[32,1,5,7168]{3,2,1,0:T(8,128)(2,1)}), bf16[32,1,5,7168]{3,2,1,0:T(8,128)(2,1)}, u32[]{:S(2)}, u32[]{:S(2)}) async-start(bf16[32,1,5,7168]{3,2,1,0:T(8,128)(2,1)} %get-tuple-element.6), calls=%async_computation.2 | async-start | bytes 7340032 | tf_op jit(solution)/shard_map/all_to_all | solution.py:35
  285.8 8.2 %copy-start.2 = (bf16[1,320,128]{2,1,0:T(8,128)(2,1)S(1)}, bf16[1,320,128]{2,1,0:T(8,128)(2,1)}, u32[]{:S(2)}) copy-start(bf16[1,320,128]{2,1,0:T(8,128)(2,1)} %param.20) | copy-start | bytes 245764
  285.8 8.2 %copy-start.3 = (bf16[1,320,128]{2,1,0:T(8,128)(2,1)S(1)}, bf16[1,320,128]{2,1,0:T(8,128)(2,1)}, u32[]{:S(2)}) copy-start(bf16[1,320,128]{2,1,0:T(8,128)(2,1)} %param.21) | copy-start | bytes 245764
  294.0 4.5 copy-start.1
  318.1 21.0 %copy-start.5 = (s32[1,128,8]{1,2,0:T(8,128)S(1)}, s32[1,128,8]{1,2,0:T(8,128)}, u32[]{:S(2)}) copy-start(s32[1,128,8]{1,2,0:T(8,128)} %param.13) | copy-start | bytes 12292
  318.1 21.0 %copy-start.7 = (f32[1,128,8]{1,2,0:T(8,128)S(1)}, f32[1,128,8]{1,2,0:T(8,128)}, u32[]{:S(2)}) copy-start(f32[1,128,8]{1,2,0:T(8,128)} %param.14) | copy-start | bytes 12292
  330.2 127.4 %all-to-all-start.4 = ((bf16[32,10,7169]{2,1,0:T(8,128)(2,1)}), bf16[32,10,7169]{2,1,0:T(8,128)(2,1)}, u32[]{:S(2)}, u32[]{:S(2)}) async-start(bf16[32,10,7169]{2,1,0:T(8,128)(2,1)} %pad_maximum_fusion), calls=%async_computation.4 | async-start | bytes 14942208 | tf_op jit(solution)/shard_map/all_to_all | solution.py:44
  350.3 128.6 %collective-permute-start = (bf16[1,128,7168]{2,1,0:T(8,128)(2,1)}, bf16[1,128,7168]{2,1,0:T(8,128)(2,1)}, u32[]{:S(2)}, u32[]{:S(2)}) collective-permute-start(bf16[1,128,7168]{2,1,0:T(8,128)(2,1)} %fusion.4), channel_id=1, source_target_pairs={{0,32},{32,64},{64,96},{96,128},{128,160},{160,192},{192,224},{224... | collective-permute-start | bytes 5505032 | tf_op jit(solution)/shard_map/ppermute | solution.py:54
  462.9 4.2 copy-start.6
  470.8 45.7 %collective-permute-start.1 = (bf16[1,128,7168]{2,1,0:T(8,128)(2,1)S(1)}, bf16[1,128,7168]{2,1,0:T(8,128)(2,1)S(1)}, u32[]{:S(2)}, u32[]{:S(2)}) collective-permute-start(bf16[1,128,7168]{2,1,0:T(8,128)(2,1)S(1)} %fusion.3), channel_id=1, source_target_pairs={{0,224},{32,0},{64,32},{96,64},{128,96},{160,128},{192,160},{224,1... | collective-permute-start | bytes 5505032 | tf_op jit(solution)/shard_map/ppermute | solution.py:54
where the time goes:
time: 528 us; the launch traced here: 521 us
  waiting for transfers between devices  314 us (59%)
  local copies, waits for them, and re-layouts  55.7 us (11%)
  blocking collectives  55.1 us (10%)
  starting transfers between devices  40 us (8%)
  matrix products  34.7 us (7%)
  other arithmetic  20.2 us (4%)
    all_to_all x2, waiting for transfers between devices, send_rows(): lax.all_to_all(jnp.repeat(buffer, slices, axis=0), 'expert', split_axis=0...  157 us
    all_to_all x1, waiting for transfers between devices, side_by_side(): lax.all_to_all(both, axis, split_axis=split_dim, concat_axis=concat_dim,...  103 us
    all_to_all x1, blocking collectives, cut_exchange(): lax.all_to_all(section, axis, split_axis=0, concat_axis=0, tiled=True)  55.1 us
    ppermute x2, waiting for transfers between devices, from_behind(): return lax.ppermute(value, axis, pairs)  41.7 us
    all_to_all x2, starting transfers between devices, send_rows(): lax.all_to_all(jnp.repeat(buffer, slices, axis=0), 'expert', split_axis=0...  16.8 us
    reshape x2, local copies, waits for them, and re-layouts, send_rows(): return received.reshape(ndev * capacity, width)  16.2 us
    all_to_all x1, waiting for transfers between devices, cut_exchange(): lax.all_to_all(section, axis, split_axis=0, concat_axis=0, tiled=True)  12.1 us
  transfers between devices with their start and end apart: 6, of which 6 were waited for; matrix products, arithmetic and copies ran while one was open for 18% of the time, Pallas kernels for 0%

commit v1 on v0

v1 whole, which is shorter than its diff:
```python
import jax
import jax.numpy as jnp
from jax import lax
from jax.experimental import pallas as pl
from jax.experimental.pallas import tpu as pltpu
from jax.sharding import PartitionSpec as P

MESH = pl.DeviceIdType.MESH
BF = jnp.bfloat16
F32 = jnp.float32

D = 7168
NC = 7
CH = D // NC
NJ = 2 * NC
TOK = 128
FFD = 128
SUB = 16
PW = 640
ROWS = 320

(Z, A_L, A_R, FA_L, FA_R, B_L, B_R, FB_L, FB_R) = range(9)
(BO_L, BO_R, BN_L, BN_R, AO_L, AO_R, AN_L, AN_R, FIN0, FIN1) = range(9, 19)
NK = 19
(DBO, DBN_L, DBN_R, DAO, DAN_L, DAN_R, DZ, WT0, WT1) = range(9)
NX = 9

RS_LAG = 12
STEPS = NJ + RS_LAG + 6


def iota(shape, dim):
    return lax.broadcasted_iota(jnp.int32, shape, dim)


def onehot(cond):
    return jnp.where(cond, 1.0, 0.0).astype(BF)


def nn(a, b):
    return jnp.dot(a, b, preferred_element_type=F32)


def nt(a, b):
    return lax.dot_general(a, b, (((1,), (1,)), ((), ())), preferred_element_type=F32)


def relay_kernel(
    act, cot, fids, fgates, bids, bgates, gw, uw, dw, gpre, upre,
    fin_out, wt_out, gg_out,
    tok, gu, wd, ids, gates, pre, pref, gbuf, zbuf, qbuf, bo, bn, ao, an, fbuf,
    lhs, pt, wts, perm_u, perm_p, xbuf, acc, accb, hid, ggu, dbuf, dbo, dbn, dao, dan, dfin, dz, ggb,
    ssem, rsem, xs, xr, lsem, osem,
):
    sec = lax.axis_index("section")
    exp = lax.axis_index("expert")
    core = lax.rem(sec, 2)
    zlo = exp // 16
    cx = lax.rem(exp // 4, 4)
    cy = lax.rem(exp, 4)
    a = cx * (1 - core) + cy * core
    b = cy * (1 - core) + cx * core
    al, ar, aopp = lax.rem(a + 3, 4), lax.rem(a + 1, 4), lax.rem(a + 2, 4)
    bl, br, bopp = lax.rem(b + 3, 4), lax.rem(b + 1, 4), lax.rem(b + 2, 4)

    def plane(ap, bp):
        return zlo * 16 + ap * (4 - 3 * core) + bp * (1 + 3 * core)

    partner = exp + 16 - 32 * zlo
    dev_al, dev_ar = {"expert": plane(al, b)}, {"expert": plane(ar, b)}
    dev_bl, dev_br = {"expert": plane(a, bl)}, {"expert": plane(a, br)}
    dev_z = {"expert": partner}
    nxt, prv = lax.rem(sec + 1, 8), lax.rem(sec + 7, 8)

    def load(src, dst, k):
        return pltpu.make_async_copy(src, dst, lsem.at[k])

    small = [
        load(fids.at[0], ids.at[0], NJ),
        load(bids.at[0], ids.at[1], NJ + 1),
        load(fgates.at[0], gates.at[0], NJ + 2),
        load(bgates.at[0], gates.at[1], NJ + 3),
    ]
    big = [
        load(gw.at[0], gu.at[:, pl.ds(0, FFD)], NJ + 4),
        load(uw.at[0], gu.at[:, pl.ds(FFD, FFD)], NJ + 5),
        load(dw.at[0], wd, NJ + 6),
        load(gpre.at[0], pre.at[:, pl.ds(0, FFD)], NJ + 7),
        load(upre.at[0], pre.at[:, pl.ds(FFD, FFD)], NJ + 8),
    ]
    toks = []
    for j in range(NJ):
        src = act if j < NC else cot
        toks.append(load(src.at[0, :, pl.ds((j % NC) * CH, CH)], tok.at[j], j))
    for c in small:
        c.start()
    for c in toks[:NC]:
        c.start()
    for c in big[:2]:
        c.start()
    for c in toks[NC:]:
        c.start()
    for c in big[2:]:
        c.start()

    barrier = pltpu.get_barrier_semaphore()
    peers = [dev_al, dev_ar, dev_bl, dev_br, dev_z]
    for s in (nxt, prv):
        peers.append({"section": s, "expert": exp})
        peers.append({"section": s, "expert": partner})
    for dev in peers:
        pl.semaphore_signal(barrier, inc=1, device_id=dev, device_id_type=MESH)

    for c in small:
        c.wait()
    lower = onehot(iota((TOK, TOK), 0) >= iota((TOK, TOK), 1))
    lane = iota((TOK, TOK), 1)
    q0 = iota((160, TOK), 0)
    spread = onehot(
        iota((160, TOK), 1) == (q0 >> 3) + jnp.where(q0 >= 80, 6, 0)
    )
    for p in range(2):
        table = jnp.zeros((TOK, TOK), F32)
        weighted = jnp.zeros((TOK, TOK), F32)
        for h in range(2):
            e = zlo if h == 0 else 1 - zlo
            match = ids[p] == e
            routed = jnp.max(jnp.where(match, 1.0, 0.0), axis=1, keepdims=True)
            w = jnp.sum(jnp.where(match, gates[p], 0.0), axis=1, keepdims=True)
            wide = jnp.broadcast_to(routed, (TOK, TOK))
            rank = nn(lower, wide.astype(BF)).astype(jnp.int32) - 1 + 16 * h
            placed = jnp.where((lane == rank) & (wide > 0.5), 1.0, 0.0)
            table = table + placed
            weighted = weighted + placed * w
        pt[p] = table.astype(BF)
        wts[p] = weighted
        lhs[p] = nt(spread, table.astype(BF)).astype(BF)
    pl.semaphore_wait(barrier, len(peers))

    def extra(src, dst, k, dev):
        return pltpu.make_async_remote_copy(
            src_ref=src, dst_ref=dst, send_sem=xs.at[k], recv_sem=xr.at[k],
            device_id=dev, device_id_type=MESH,
        )

    wt_copies = [
        extra(wts.at[0], wt_out.at[0], WT0, {"section": nxt, "expert": exp}),
        extra(wts.at[1], wt_out.at[1], WT1, {"section": prv, "expert": exp}),
    ]
    for c in wt_copies:
        c.start()

    def ring(src, dst, k, j, dev):
        return pltpu.make_async_remote_copy(
            src_ref=src, dst_ref=dst, send_sem=ssem.at[k, j], recv_sem=rsem.at[k, j],
            device_id=dev, device_id_type=MESH,
        )

    def out(k, j):
        if k == Z:
            return ring(zbuf.at[j], gbuf.at[j, b, a, 1], k, j, dev_z)
        if k == A_L:
            return ring(gbuf.at[j, b, a], gbuf.at[j, b, a], k, j, dev_ar)
        if k == A_R:
            return ring(gbuf.at[j, b, a], gbuf.at[j, b, a], k, j, dev_al)
        if k == FA_L:
            return ring(gbuf.at[j, b, al, 0], gbuf.at[j, b, al, 0], k, j, dev_ar)
        if k == FA_R:
            return ring(gbuf.at[j, b, ar, 1], gbuf.at[j, b, ar, 1], k, j, dev_al)
        if k == B_L:
            return ring(gbuf.at[j, b], gbuf.at[j, b], k, j, dev_br)
        if k == B_R:
            return ring(gbuf.at[j, b], gbuf.at[j, b], k, j, dev_bl)
        if k == FB_L:
            half = gbuf.at[j, bl, pl.ds(0, 2)]
            return ring(half, half, k, j, dev_br)
        if k == FB_R:
            half = gbuf.at[j, br, pl.ds(2, 2)]
            return ring(half, half, k, j, dev_bl)
        if k == BO_L:
            return ring(qbuf.at[j, bopp, pl.ds(0, 2)], bo.at[j, 0], k, j, dev_br)
        if k == BO_R:
            return ring(qbuf.at[j, bopp, pl.ds(2, 2)], bo.at[j, 1], k, j, dev_bl)
        if k == BN_L:
            return ring(qbuf.at[j, br], bn.at[j, 0], k, j, dev_br)
        if k == BN_R:
            return ring(qbuf.at[j, bl], bn.at[j, 1], k, j, dev_bl)
        if k == AO_L:
            return ring(qbuf.at[j, b, aopp, 0], ao.at[j, 0], k, j, dev_ar)
        if k == AO_R:
            return ring(qbuf.at[j, b, aopp, 1], ao.at[j, 1], k, j, dev_al)
        if k == AN_L:
            return ring(qbuf.at[j, b, ar], an.at[j, 0], k, j, dev_ar)
        if k == AN_R:
            return ring(qbuf.at[j, b, al], an.at[j, 1], k, j, dev_al)
        to = jnp.where(j < NC, nxt, prv)
        h = k - FIN0
        dev = {"section": to, "expert": exp if h == 0 else partner}
        return ring(fbuf.at[j, h], fin_out.at[j, h], k, j, dev)

    def arrived(k, j):
        dst = {
            Z: lambda: gbuf.at[j, b, a, 1],
            A_L: lambda: gbuf.at[j, b, al],
            A_R: lambda: gbuf.at[j, b, ar],
            FA_L: lambda: gbuf.at[j, b, aopp, 0],
            FA_R: lambda: gbuf.at[j, b, aopp, 1],
            B_L: lambda: gbuf.at[j, bl],
            B_R: lambda: gbuf.at[j, br],
            FB_L: lambda: gbuf.at[j, bopp, pl.ds(0, 2)],
            FB_R: lambda: gbuf.at[j, bopp, pl.ds(2, 2)],
            BO_L: lambda: bo.at[j, 0],
            BO_R: lambda: bo.at[j, 1],
            BN_L: lambda: bn.at[j, 0],
            BN_R: lambda: bn.at[j, 1],
            AO_L: lambda: ao.at[j, 0],
            AO_R: lambda: ao.at[j, 1],
            AN_L: lambda: an.at[j, 0],
            AN_R: lambda: an.at[j, 1],
            FIN0: lambda: fin_out.at[j, 0],
            FIN1: lambda: fin_out.at[j, 1],
        }[k]()
        ring(dst, dst, k, j, dev_z).wait_recv()

    def send(*kinds, j):
        for k in kinds:
            out(k, j).start()

    def sent(*kinds, j):
        for k in kinds:
            out(k, j).wait_send()

    row_k = iota((SUB, FFD), 0) & 7

    def pack(j):
        p = j // NC
        load(act.at[0, :, pl.ds(0, CH)], tok.at[j], j).wait()
        y = nn(lhs[p], tok[j])
        for h in range(2):
            for c in range(5):
                r = (h * 5 + c) * SUB
                v = y[r:r + SUB, 0:FFD]
                for k in range(1, 8):
                    v = jnp.where(row_k == k, y[r:r + SUB, k * FFD:(k + 1) * FFD], v)
                if h == 0:
                    gbuf[j, b, a, 0, :, c * FFD:(c + 1) * FFD] = v.astype(BF)
                else:
                    zbuf[j, :, c * FFD:(c + 1) * FFD] = v.astype(BF)

    def tables():
        o = iota((256, 256), 0)
        i = iota((256, 256), 1)
        perm_u[...] = onehot(i == ((o & 31) >> 1) * 16 + (o & 1) * 8 + (o >> 5))
        perm_p[...] = onehot(o == ((i & 31) >> 1) * 16 + (i & 1) * 8 + (i >> 5))

    def saved():
        for c in big[3:]:
            c.wait()
        i = iota((ROWS, ROWS), 0)
        hc = i >> 5
        h = jnp.where(hc >= 5, 1, 0)
        c5 = hc - 5 * h
        bp = (i >> 3) & 3
        ap = (i >> 1) & 3
        xy = ap * (4 - 3 * core) + bp * (1 + 3 * core)
        pln = zlo + h - 2 * zlo * h
        src = (pln * 16 + xy) * 10 + c5 * 2 + (i & 1)
        pref[...] = nn(onehot(iota((ROWS, ROWS), 1) == src), pre[...])

    def unpack(j):
        for h in range(2):
            g = gbuf[j, :, :, h].reshape(256, PW)
            r = nn(perm_u[...], g).astype(BF)
            for c in range(5):
                for k in range(8):
                    xbuf[(h * 5 + c) * 32:(h * 5 + c) * 32 + 32, k * FFD:(k + 1) * FFD] = (
                        r[k * 32:(k + 1) * 32, c * FFD:(c + 1) * FFD]
                    )

    def repack(j, o):
        o = o.astype(BF)
        for h in range(2):
            cols = []
            for c in range(5):
                r0 = (h * 5 + c) * 32
                cols.append(
                    jnp.concatenate(
                        [o[r0:r0 + 32, k * FFD:(k + 1) * FFD] for k in range(8)], axis=0
                    )
                )
            r = jnp.concatenate(cols, axis=1)
            q = nn(perm_p[...], r).astype(BF)
            qbuf[j, :, :, h] = q.reshape(4, 4, SUB, PW)

    def forward_rows(j):
        i = pl.multiple_of(j * CH, CH)

        @pl.when(j == 0)
        def _():
            for c in big[:2]:
                c.wait()
            acc[...] = nn(xbuf[...], gu[pl.ds(i, CH), :])

        @pl.when(j > 0)
        def _():
            acc[...] += nn(xbuf[...], gu[pl.ds(i, CH), :])

        @pl.when(j == NC - 1)
        def _():
            big[2].wait()
            g = acc[:, 0:FFD]
            hid[...] = (g / (1.0 + jnp.exp(-g)) * acc[:, FFD:2 * FFD]).astype(BF)

    def backward_rows(j):
        i = pl.multiple_of((j - NC) * CH, CH)

        @pl.when(j == NC)
        def _():
            accb[...] = nt(xbuf[...], wd[:, pl.ds(i, CH)])

        @pl.when(j > NC)
        def _():
            accb[...] += nt(xbuf[...], wd[:, pl.ds(i, CH)])

        @pl.when(j == NJ - 1)
        def _():
            gh = accb[...]
            g = pref[:, 0:FFD]
            u = pref[:, FFD:2 * FFD]
            s = 1.0 / (1.0 + jnp.exp(-g))
            silu = g * s
            ggu[:, 0:FFD] = (gh * u * s * (1.0 + g * (1.0 - s))).astype(BF)
            ggu[:, FFD:2 * FFD] = (gh * silu).astype(BF)
            dots = jnp.sum(gh * silu * u, axis=1, keepdims=True)
            at = iota((ROWS, FFD), 1) == (iota((ROWS, FFD), 0) >> 5)
            spot = jnp.where(at, jnp.broadcast_to(dots, (ROWS, FFD)), 0.0).astype(BF)
            o = iota((FFD, ROWS), 0)
            i2 = iota((FFD, ROWS), 1) & 31
            pick = onehot(((o & 7) < 2) & (i2 == (o >> 3) * 2 + (o & 7)))
            dbuf[...] = nn(pick, spot).reshape(4, 4, 8, FFD)

    def f32(v):
        return v.astype(F32)

    @pl.loop(0, STEPS)
    def _(t):
        def event(lag, lo=0, hi=NJ):
            def wrap(f):
                @pl.when((t - lag >= lo) & (t - lag < hi))
                def _():
                    f(t - lag)
            return wrap

        @event(0)
        def _(j):
            pack(j)
            send(Z, j=j)

            @pl.when(j == 1)
            def _():
                tables()

        @event(1)
        def _(j):
            arrived(Z, j)
            send(A_L, A_R, j=j)

        @event(2)
        def _(j):
            arrived(A_L, j)
            send(FA_L, j=j)
            arrived(A_R, j)
            send(FA_R, j=j)

        @event(3)
        def _(j):
            arrived(FA_L, j)
            arrived(FA_R, j)
            send(B_L, B_R, j=j)

        @event(4)
        def _(j):
            arrived(B_L, j)
            send(FB_L, j=j)
            arrived(B_R, j)
            send(FB_R, j=j)

        @event(RS_LAG)
        def _(j):
            @pl.when(j < NC)
            def _():
                i = pl.multiple_of(j * CH, CH)
                repack(j, nn(hid[...], wd[:, pl.ds(i, CH)]))

            @pl.when(j >= NC)
            def _():
                i = pl.multiple_of((j - NC) * CH, CH)
                repack(j, nt(ggu[...], gu[pl.ds(i, CH), :]))

            send(BO_L, BO_R, j=j)

            @pl.when(j == NC)
            def _():
                extra(dbuf.at[bopp], dbo, DBO, dev_br).start()

        @event(RS_LAG + 1)
        def _(j):
            arrived(BO_L, j)
            qbuf[j, br, 0:2] = (f32(qbuf[j, br, 0:2]) + f32(bo[j, 0])).astype(BF)
            send(BN_L, j=j)
            arrived(BO_R, j)
            qbuf[j, bl, 2:4] = (f32(qbuf[j, bl, 2:4]) + f32(bo[j, 1])).astype(BF)
            send(BN_R, j=j)

            @pl.when(j == NC)
            def _():
                extra(dbuf.at[bopp], dbo, DBO, dev_br).wait()
                dbuf[br] = dbuf[br] + dbo[...]
                extra(dbuf.at[br], dbn.at[0], DBN_L, dev_br).start()
                extra(dbuf.at[bl], dbn.at[1], DBN_R, dev_bl).start()

        @event(RS_LAG + 2)
        def _(j):
            arrived(BN_L, j)
            arrived(BN_R, j)
            qbuf[j, b] = (f32(qbuf[j, b]) + f32(bn[j, 0]) + f32(bn[j, 1])).astype(BF)
            send(AO_L, AO_R, j=j)

            @pl.when(j == NC)
            def _():
                extra(dbuf.at[br], dbn.at[0], DBN_L, dev_br).wait()
                extra(dbuf.at[bl], dbn.at[1], DBN_R, dev_bl).wait()
                dbuf[b] = dbuf[b] + dbn[0] + dbn[1]
                extra(dbuf.at[b, aopp], dao, DAO, dev_ar).start()

        @event(RS_LAG + 3)
        def _(j):
            arrived(AO_L, j)
            qbuf[j, b, ar, 0] = (f32(qbuf[j, b, ar, 0]) + f32(ao[j, 0])).astype(BF)
            send(AN_L, j=j)
            arrived(AO_R, j)
            qbuf[j, b, al, 1] = (f32(qbuf[j, b, al, 1]) + f32(ao[j, 1])).astype(BF)
            send(AN_R, j=j)

            @pl.when(j == NC)
            def _():
                extra(dbuf.at[b, aopp], dao, DAO, dev_ar).wait()
                dbuf[b, ar] = dbuf[b, ar] + dao[...]
                extra(dbuf.at[b, ar], dan.at[0], DAN_L, dev_ar).start()
                extra(dbuf.at[b, al], dan.at[1], DAN_R, dev_al).start()

        @event(RS_LAG + 4)
        def _(j):
            arrived(AN_L, j)
            arrived(AN_R, j)
            fbuf[j] = (f32(qbuf[j, b, a]) + f32(an[j, 0]) + f32(an[j, 1])).astype(BF)
            send(FIN0, FIN1, j=j)

            @pl.when(j == NC)
            def _():
                extra(dbuf.at[b, ar], dan.at[0], DAN_L, dev_ar).wait()
                extra(dbuf.at[b, al], dan.at[1], DAN_R, dev_al).wait()
                dfin[...] = dbuf[b, a] + dan[0] + dan[1]
                extra(dfin, dz, DZ, dev_z).start()

        @event(RS_LAG + 5)
        def _(j):
            arrived(FIN0, j)
            arrived(FIN1, j)
            sent(BO_L, BO_R, BN_L, BN_R, AO_L, AO_R, AN_L, AN_R, FIN0, FIN1, j=j)

            @pl.when(j == NC)
            def _():
                extra(dfin, dz, DZ, dev_z).wait()
                la = iota((8, FFD), 1)
                mine = jnp.where(la < 5, dfin[...], dz[...])
                i = iota((TOK, TOK), 0)
                l = iota((TOK, TOK), 1)
                total = jnp.zeros((TOK, TOK), F32)
                for par in range(2):
                    h = i >> 4
                    ok = (i < 32) & ((i & 1) == par) & ((i & 15) < 10)
                    to = onehot(ok & (l == h * 5 + ((i & 15) >> 1)))
                    total = total + nn(pt[1], to) * mine[par:par + 1, :]
                d0 = jnp.sum(jnp.where(l < 5, total, 0.0), axis=1, keepdims=True)
                d1 = jnp.sum(jnp.where(l >= 5, total, 0.0), axis=1, keepdims=True)
                which = ids[1]
                ggb[...] = jnp.where(which == zlo, d0, 0.0) + jnp.where(
                    which == 1 - zlo, d1, 0.0
                )
                pltpu.make_async_copy(ggb, gg_out, osem).start()

        @event(5)
        def _(j):
            @pl.when(j == 0)
            def _():
                saved()

            arrived(FB_L, j)
            arrived(FB_R, j)
            unpack(j)

            @pl.when(j < NC)
            def _():
                forward_rows(j)

            @pl.when(j >= NC)
            def _():
                backward_rows(j)

            sent(Z, A_L, A_R, FA_L, FA_R, B_L, B_R, FB_L, FB_R, j=j)

    for c in wt_copies:
        c.wait()
    pltpu.make_async_copy(ggb, gg_out, osem).wait()


def relay(*args):
    any_spec = pl.BlockSpec(memory_space=pl.ANY)
    vmem = pltpu.VMEM
    return pl.pallas_call(
        relay_kernel,
        out_shape=(
            jax.ShapeDtypeStruct((NJ, 2, SUB, PW), BF),
            jax.ShapeDtypeStruct((2, TOK, TOK), F32),
            jax.ShapeDtypeStruct((TOK, 8), F32),
        ),
        in_specs=[any_spec] * 11,
        out_specs=(any_spec,) * 3,
        scratch_shapes=[
            vmem((NJ, TOK, CH), BF),
            vmem((D, 2 * FFD), BF),
            vmem((FFD, D), BF),
            vmem((2, TOK, 8), jnp.int32),
            vmem((2, TOK, 8), F32),
            vmem((ROWS, 2 * FFD), BF),
            vmem((ROWS, 2 * FFD), F32),
            vmem((NJ, 4, 4, 2, SUB, PW), BF),
            vmem((NJ, SUB, PW), BF),
            vmem((NJ, 4, 4, 2, SUB, PW), BF),
            vmem((NJ, 2, 2, 2, SUB, PW), BF),
            vmem((NJ, 2, 4, 2, SUB, PW), BF),
            vmem((NJ, 2, SUB, PW), BF),
            vmem((NJ, 2, 2, SUB, PW), BF),
            vmem((NJ, 2, SUB, PW), BF),
            vmem((2, 160, TOK), BF),
            vmem((2, TOK, TOK), BF),
            vmem((2, TOK, TOK), F32),
            vmem((256, 256), BF),
            vmem((256, 256), BF),
            vmem((ROWS, CH), BF),
            vmem((ROWS, 2 * FFD), F32),
            vmem((ROWS, FFD), F32),
            vmem((ROWS, FFD), BF),
            vmem((ROWS, 2 * FFD), BF),
            vmem((4, 4, 8, FFD), F32),
            vmem((4, 8, FFD), F32),
            vmem((2, 4, 8, FFD), F32),
            vmem((8, FFD), F32),
            vmem((2, 8, FFD), F32),
            vmem((8, FFD), F32),
            vmem((8, FFD), F32),
            vmem((TOK, 8), F32),
            pltpu.SemaphoreType.DMA((NK, NJ)),
            pltpu.SemaphoreType.DMA((NK, NJ)),
            pltpu.SemaphoreType.DMA((NX,)),
            pltpu.SemaphoreType.DMA((NX,)),
            pltpu.SemaphoreType.DMA((NJ + 9,)),
            pltpu.SemaphoreType.DMA,
        ],
        compiler_params=pltpu.CompilerParams(
            collective_id=0, has_side_effects=True, vmem_limit_bytes=62 * 2**20
        ),
        name="relay",
    )(*args)


def spread_kernel(ff, fb, wt, gg, next_ref, prev_ref, gg_ref, sel, lhs):
    @pl.when(pl.program_id(0) == 0)
    def _():
        gg_ref[0] = gg[...]
        o = iota((256, 160), 0)
        v = iota((256, 160), 1)
        slot = (v >> 3) + jnp.where(v >= 80, 6, 0)
        sel[...] = onehot(((v & 7) == (o >> 5)) & ((o & 31) == slot))
        for p in range(2):
            w = wt[p][:, 0:32]
            hi = w.astype(BF)
            lhs[p, :, 0:32] = hi
            lhs[p, :, 32:64] = (w - hi.astype(F32)).astype(BF)

    for p, (src, dst) in enumerate(((ff, next_ref), (fb, prev_ref))):
        v = jnp.concatenate(
            [src[0, h, :, c * FFD:(c + 1) * FFD] for h in range(2) for c in range(5)], axis=0
        )
        u = nn(sel[...], v).astype(BF)
        row = jnp.concatenate([u[k * 32:(k + 1) * 32] for k in range(8)], axis=1)
        both = jnp.concatenate([row, row], axis=0)
        dst[0] = nn(lhs[p], both).astype(BF)


def dense(fin, wt, gg):
    return pl.pallas_call(
        spread_kernel,
        grid=(NC,),
        out_shape=(
            jax.ShapeDtypeStruct((1, TOK, D), BF),
            jax.ShapeDtypeStruct((1, TOK, D), BF),
            jax.ShapeDtypeStruct((1, TOK, 8), F32),
        ),
        in_specs=[
            pl.BlockSpec((1, 2, SUB, PW), lambda i: (i, 0, 0, 0)),
            pl.BlockSpec((1, 2, SUB, PW), lambda i: (i + NC, 0, 0, 0)),
            pl.BlockSpec((2, TOK, TOK), lambda i: (0, 0, 0)),
            pl.BlockSpec((TOK, 8), lambda i: (0, 0)),
        ],
        out_specs=(
            pl.BlockSpec((1, TOK, CH), lambda i: (0, 0, i)),
            pl.BlockSpec((1, TOK, CH), lambda i: (0, 0, i)),
            pl.BlockSpec((1, TOK, 8), lambda i: (0, 0, 0)),
        ),
        scratch_shapes=[pltpu.VMEM((256, 160), BF), pltpu.VMEM((2, TOK, 64), BF)],
        name="dense",
    )(fin, fin, wt, gg)


def body(*args):
    fin, wt, gg = relay(*args)
    return dense(fin, wt, gg)


def solution(mesh):
    rows = P("section", "expert", None)
    cols = P("section", None, "expert")
    return jax.shard_map(
        body,
        mesh=mesh,
        in_specs=(rows,) * 6 + (cols, cols, rows, cols, cols),
        out_specs=(rows,) * 3,
        check_vma=False,
    )
```

time: 528 us -> 152 us (0.29); the launches traced: 521 us -> 151 us
  waiting for transfers between devices: 314 us -> 0 us
  Pallas kernels: 0 us -> 144 us
  blocking collectives: 55.1 us -> 0 us
  local copies, waits for them, and re-layouts: 55.7 us -> 7.16 us
  starting transfers between devices: 40 us -> 0 us
  matrix products: 34.7 us -> 0 us
  other arithmetic: 20.2 us -> 0 us
    all_to_all x4 -> x0, waiting for transfers between devices: 272 us -> none  [the longest x2 157 us: send_rows(): lax.all_to_all(jnp.repeat(buffer, slices, axis=0), 'expert', split_axis=0...]
    pallas_call x0 -> x2, Pallas kernels: none -> 144 us  [the longest x1 137 us: relay(): pl.pallas_call(relay_kernel, out_shape=(jax.ShapeDtypeStruct((NJ, 2, SUB,...]
    all_to_all x1 -> x0, blocking collectives: 55.1 us -> none  [cut_exchange(): lax.all_to_all(section, axis, split_axis=0, concat_axis=0, tiled=True)]
    ppermute x2 -> x0, waiting for transfers between devices: 41.7 us -> none  [from_behind(): return lax.ppermute(value, axis, pairs)]
    dot_general x10 -> x0, matrix products: 34.7 us -> none  [the longest x1 10 us: body(): jnp.dot(hidden, w_down, preferred_element_type=jnp.float32)]
    all_to_all x4 -> x0, starting transfers between devices: 31.5 us -> none  [the longest x2 16.8 us: send_rows(): lax.all_to_all(jnp.repeat(buffer, slices, axis=0), 'expert', split_axis=0...]
    reshape x3 -> x0, local copies, waits for them, and re-layouts: 24 us -> none  [the longest x2 16.2 us: send_rows(): return received.reshape(ndev * capacity, width)]
    concatenate x2 -> x0, other arithmetic: 12.4 us -> none  [the longest x1 6.8 us: side_by_side(): jnp.concatenate([a.reshape(*a.shape[:along], w) for a, w in zip(arrays, w...]
  transfers between devices with their start and end apart: 6 -> 0, of which waited for: 6 -> 0; matrix products, arithmetic and copies ran while one was open for 18% -> 0% of each run, Pallas kernels for 0% -> 0%
where the time goes in v1:
time: 152 us; the launch traced here: 151 us
  Pallas kernels  144 us (95%)
  local copies, waits for them, and re-layouts  7.16 us (5%)
    pallas_call x1, Pallas kernels, relay(): pl.pallas_call(relay_kernel, out_shape=(jax.ShapeDtypeStruct((NJ, 2, SUB,...  137 us
    pallas_call x1, Pallas kernels, dense(): pl.pallas_call(spread_kernel, grid=(NC,), out_shape=(jax.ShapeDtypeStruct...  7 us
    unnamed x4, local copies, waits for them, and re-layouts  5.66 us

profile of v1, /device:TPU:1, one launch (start us, length us, event | category | flops | bytes accessed | tf_op | source)
XLA Modules:
  0.0 151.5 jit_solution(230105135118376465)
XLA Ops:
  0.6 1.4 copy.14.fids
  2.0 1.4 copy.15.fgates
  3.5 1.4 copy.16.bids
  4.9 1.4 copy.17.bgates
  6.3 136.7 %relay.1 = (bf16[14,2,16,640]{3,2,1,0:T(8,128)(2,1)}, f32[2,128,128]{2,1,0:T(8,128)}, f32[128,8]{1,0:T(8,128)}) custom-call(bf16[1,128,7168]{2,1,0:T(8,128)(2,1)} %act.1, bf16[1,128,7168]{2,1,0:T(8,128)(2,1)} %cot.1, s32[1,128,8]{2,1,0:T(8,128)} %copy.14.fids, f32[1,128,8]{2,1,0:T(8,128)} %copy.15.fgates, s32[1,128,8]{2,1,0:T(8,128)} %copy.16.bids, ...), custom_call_target="tpu_custom_call" | custom-call | tf_op jit(solution)/shard_map/relay/pallas_call | solution.py:521
  143.0 7.0 %dense.1 = (bf16[1,128,7168]{2,1,0:T(8,128)(2,1)}, bf16[1,128,7168]{2,1,0:T(8,128)(2,1)}, f32[1,128,8]{2,1,0:T(8,128)}) custom-call(bf16[14,2,16,640]{3,2,1,0:T(8,128)(2,1)} %get-tuple-element.6.ff.fb, bf16[14,2,16,640]{3,2,1,0:T(8,128)(2,1)} %get-tuple-element.6.ff.fb, f32[2,128,128]{2,1,0:T(8,128)} %get-tuple-element.7.wt, f32[128,8]{1,0:T(8,128)} %get-tuple-element.8.gg), custom_call_target="tpu_custom_call" | custom-call | tf_op jit(solution)/shard_map/dense/pallas_call | solution.py:603
  150.0 1.5 copy.18

commit v2 on v1

--- a/solution.py
+++ b/solution.py
@@ -25,8 +25,10 @@
 (DBO, DBN_L, DBN_R, DAO, DAN_L, DAN_R, DZ, WT0, WT1) = range(9)
 NX = 9
 
-RS_LAG = 12
-STEPS = NJ + RS_LAG + 6
+E1, E2, E3, E4, E5 = 1, 3, 5, 7, 9
+R0 = E5 + NC
+R1, R2, R3, R4, R5 = R0 + 2, R0 + 4, R0 + 6, R0 + 8, R0 + 10
+STEPS = NJ + R5
 
 
 def iota(shape, dim):
@@ -47,10 +49,10 @@
 
 def relay_kernel(
     act, cot, fids, fgates, bids, bgates, gw, uw, dw, gpre, upre,
-    fin_out, wt_out, gg_out,
-    tok, gu, wd, ids, gates, pre, pref, gbuf, zbuf, qbuf, bo, bn, ao, an, fbuf,
-    lhs, pt, wts, perm_u, perm_p, xbuf, acc, accb, hid, ggu, dbuf, dbo, dbn, dao, dan, dfin, dz, ggb,
-    ssem, rsem, xs, xr, lsem, osem,
+    u_out, wt_out, gg_out,
+    tok, gu, wd, ids, gates, pre, pref, gbuf, zbuf, qbuf, bo, bn, ao, an, fbuf, fin, ubuf, sel,
+    lhs, rk, wts, perm_u, perm_p, xbuf, acc, accb, hid, ggu, dbuf, dbo, dbn, dao, dan, dfin, dz, ggb,
+    ssem, rsem, xs, xr, lsem, osem, usem,
 ):
     sec = lax.axis_index("section")
     exp = lax.axis_index("expert")
@@ -113,28 +115,24 @@
 
     for c in small:
         c.wait()
-    lower = onehot(iota((TOK, TOK), 0) >= iota((TOK, TOK), 1))
-    lane = iota((TOK, TOK), 1)
-    q0 = iota((160, TOK), 0)
-    spread = onehot(
-        iota((160, TOK), 1) == (q0 >> 3) + jnp.where(q0 >= 80, 6, 0)
-    )
+    upper = onehot(iota((TOK, TOK), 0) <= iota((TOK, TOK), 1))
+    slot16 = iota((16, TOK), 0)
+    row160 = iota((160, TOK), 0)
     for p in range(2):
-        table = jnp.zeros((TOK, TOK), F32)
-        weighted = jnp.zeros((TOK, TOK), F32)
+        ranks = []
         for h in range(2):
             e = zlo if h == 0 else 1 - zlo
             match = ids[p] == e
-            routed = jnp.max(jnp.where(match, 1.0, 0.0), axis=1, keepdims=True)
-            w = jnp.sum(jnp.where(match, gates[p], 0.0), axis=1, keepdims=True)
-            wide = jnp.broadcast_to(routed, (TOK, TOK))
-            rank = nn(lower, wide.astype(BF)).astype(jnp.int32) - 1 + 16 * h
-            placed = jnp.where((lane == rank) & (wide > 0.5), 1.0, 0.0)
-            table = table + placed
-            weighted = weighted + placed * w
-        pt[p] = table.astype(BF)
-        wts[p] = weighted
-        lhs[p] = nt(spread, table.astype(BF)).astype(BF)
+            routed = jnp.max(jnp.where(match, 1.0, 0.0), axis=0, keepdims=True)
+            w = jnp.sum(jnp.where(match, gates[p], 0.0), axis=0, keepdims=True)
+            count = nn(jnp.broadcast_to(routed, (8, TOK)).astype(BF), upper)
+            rank = jnp.where(routed > 0.5, count.astype(jnp.int32) - 1, -1)
+            rk[p, h] = rank
+            wts[p, h * 16:h * 16 + 16] = jnp.where(slot16 == rank[0:1], w, 0.0)
+            ranks.append(rank[0:1])
+        low = (row160 >> 3) == ranks[0]
+        high = ((row160 >> 3) - 10) == ranks[1]
+        lhs[p] = jnp.where(row160 < 80, jnp.where(low, 1.0, 0.0), jnp.where(high, 1.0, 0.0)).astype(BF)
     pl.semaphore_wait(barrier, len(peers))
 
     def extra(src, dst, k, dev):
@@ -196,7 +194,7 @@
         to = jnp.where(j < NC, nxt, prv)
         h = k - FIN0
         dev = {"section": to, "expert": exp if h == 0 else partner}
-        return ring(fbuf.at[j, h], fin_out.at[j, h], k, j, dev)
+        return ring(fbuf.at[j, h], fin.at[j, h], k, j, dev)
 
     def arrived(k, j):
         dst = {
@@ -217,8 +215,8 @@
             AO_R: lambda: ao.at[j, 1],
             AN_L: lambda: an.at[j, 0],
             AN_R: lambda: an.at[j, 1],
-            FIN0: lambda: fin_out.at[j, 0],
-            FIN1: lambda: fin_out.at[j, 1],
+            FIN0: lambda: fin.at[j, 0],
+            FIN1: lambda: fin.at[j, 1],
         }[k]()
         ring(dst, dst, k, j, dev_z).wait_recv()
 
@@ -252,6 +250,10 @@
         i = iota((256, 256), 1)
         perm_u[...] = onehot(i == ((o & 31) >> 1) * 16 + (o & 1) * 8 + (o >> 5))
         perm_p[...] = onehot(o == ((i & 31) >> 1) * 16 + (i & 1) * 8 + (i >> 5))
+        o = iota((256, 160), 0)
+        v = iota((256, 160), 1)
+        slot = (v >> 3) + jnp.where(v >= 80, 6, 0)
+        sel[...] = onehot(((v & 7) == (o >> 5)) & ((o & 31) == slot))
 
     def saved():
         for c in big[3:]:
@@ -360,32 +362,32 @@
             def _():
                 tables()
 
-        @event(1)
+        @event(E1)
         def _(j):
             arrived(Z, j)
             send(A_L, A_R, j=j)
 
-        @event(2)
+        @event(E2)
         def _(j):
             arrived(A_L, j)
             send(FA_L, j=j)
             arrived(A_R, j)
             send(FA_R, j=j)
 
-        @event(3)
+        @event(E3)
         def _(j):
             arrived(FA_L, j)
             arrived(FA_R, j)
             send(B_L, B_R, j=j)
 
-        @event(4)
+        @event(E4)
         def _(j):
             arrived(B_L, j)
             send(FB_L, j=j)
             arrived(B_R, j)
             send(FB_R, j=j)
 
-        @event(RS_LAG)
+        @event(R0)
         def _(j):
             @pl.when(j < NC)
             def _():
@@ -403,7 +405,7 @@
             def _():
                 extra(dbuf.at[bopp], dbo, DBO, dev_br).start()
 
-        @event(RS_LAG + 1)
+        @event(R1)
         def _(j):
             arrived(BO_L, j)
             qbuf[j, br, 0:2] = (f32(qbuf[j, br, 0:2]) + f32(bo[j, 0])).astype(BF)
@@ -419,7 +421,7 @@
                 extra(dbuf.at[br], dbn.at[0], DBN_L, dev_br).start()
                 extra(dbuf.at[bl], dbn.at[1], DBN_R, dev_bl).start()
 
-        @event(RS_LAG + 2)
+        @event(R2)
         def _(j):
             arrived(BN_L, j)
             arrived(BN_R, j)
@@ -433,7 +435,7 @@
                 dbuf[b] = dbuf[b] + dbn[0] + dbn[1]
                 extra(dbuf.at[b, aopp], dao, DAO, dev_ar).start()
 
-        @event(RS_LAG + 3)
+        @event(R3)
         def _(j):
             arrived(AO_L, j)
             qbuf[j, b, ar, 0] = (f32(qbuf[j, b, ar, 0]) + f32(ao[j, 0])).astype(BF)
@@ -449,7 +451,7 @@
                 extra(dbuf.at[b, ar], dan.at[0], DAN_L, dev_ar).start()
                 extra(dbuf.at[b, al], dan.at[1], DAN_R, dev_al).start()
 
-        @event(RS_LAG + 4)
+        @event(R4)
         def _(j):
             arrived(AN_L, j)
             arrived(AN_R, j)
@@ -463,34 +465,41 @@
                 dfin[...] = dbuf[b, a] + dan[0] + dan[1]
                 extra(dfin, dz, DZ, dev_z).start()
 
-        @event(RS_LAG + 5)
+        @event(R5)
         def _(j):
             arrived(FIN0, j)
             arrived(FIN1, j)
+            v = jnp.concatenate(
+                [fin[j, h, :, c * FFD:(c + 1) * FFD] for h in range(2) for c in range(5)], axis=0
+            )
+            u = nn(sel[...], v).astype(BF)
+            for k in range(8):
+                ubuf[j, :, k * FFD:(k + 1) * FFD] = u[k * 32:(k + 1) * 32]
+            pltpu.make_async_copy(ubuf.at[j], u_out.at[j], usem.at[j]).start()
             sent(BO_L, BO_R, BN_L, BN_R, AO_L, AO_R, AN_L, AN_R, FIN0, FIN1, j=j)
 
             @pl.when(j == NC)
             def _():
                 extra(dfin, dz, DZ, dev_z).wait()
                 la = iota((8, FFD), 1)
-                mine = jnp.where(la < 5, dfin[...], dz[...])
-                i = iota((TOK, TOK), 0)
-                l = iota((TOK, TOK), 1)
-                total = jnp.zeros((TOK, TOK), F32)
+                mine = jnp.where(la < 5, dfin[...], dz[...]).T
+                r16 = iota((16, TOK), 0)
+                s16 = jnp.where(r16 < 5, r16, r16 - 5) * 2
+                total = jnp.zeros((16, TOK), F32)
                 for par in range(2):
-                    h = i >> 4
-                    ok = (i < 32) & ((i & 1) == par) & ((i & 15) < 10)
-                    to = onehot(ok & (l == h * 5 + ((i & 15) >> 1)))
-                    total = total + nn(pt[1], to) * mine[par:par + 1, :]
-                d0 = jnp.sum(jnp.where(l < 5, total, 0.0), axis=1, keepdims=True)
-                d1 = jnp.sum(jnp.where(l >= 5, total, 0.0), axis=1, keepdims=True)
+                    hit0 = jnp.where(rk[1, 0, 0:1] == s16 + par, 1.0, 0.0)
+                    hit1 = jnp.where(rk[1, 1, 0:1] == s16 + par, 1.0, 0.0)
+                    hit = jnp.where(r16 < 5, hit0, hit1)
+                    total = total + hit * mine[0:16, par:par + 1]
+                d0 = jnp.sum(jnp.where(r16 < 5, total, 0.0), axis=0, keepdims=True)
+                d1 = jnp.sum(jnp.where((r16 >= 5) & (r16 < 10), total, 0.0), axis=0, keepdims=True)
                 which = ids[1]
                 ggb[...] = jnp.where(which == zlo, d0, 0.0) + jnp.where(
                     which == 1 - zlo, d1, 0.0
                 )
                 pltpu.make_async_copy(ggb, gg_out, osem).start()
 
-        @event(5)
+        @event(E5)
         def _(j):
             @pl.when(j == 0)
             def _():
@@ -513,6 +522,8 @@
     for c in wt_copies:
         c.wait()
     pltpu.make_async_copy(ggb, gg_out, osem).wait()
+    for j in range(NJ):
+        pltpu.make_async_copy(ubuf.at[j], u_out.at[j], usem.at[j]).wait()
 
 
 def relay(*args):
@@ -521,9 +532,9 @@
     return pl.pallas_call(
         relay_kernel,
         out_shape=(
-            jax.ShapeDtypeStruct((NJ, 2, SUB, PW), BF),
-            jax.ShapeDtypeStruct((2, TOK, TOK), F32),
-            jax.ShapeDtypeStruct((TOK, 8), F32),
+            jax.ShapeDtypeStruct((NJ, 32, CH), BF),
+            jax.ShapeDtypeStruct((2, 32, TOK), F32),
+            jax.ShapeDtypeStruct((8, TOK), F32),
         ),
         in_specs=[any_spec] * 11,
         out_specs=(any_spec,) * 3,
@@ -531,8 +542,8 @@
             vmem((NJ, TOK, CH), BF),
             vmem((D, 2 * FFD), BF),
             vmem((FFD, D), BF),
-            vmem((2, TOK, 8), jnp.int32),
-            vmem((2, TOK, 8), F32),
+            vmem((2, 8, TOK), jnp.int32),
+            vmem((2, 8, TOK), F32),
             vmem((ROWS, 2 * FFD), BF),
             vmem((ROWS, 2 * FFD), F32),
             vmem((NJ, 4, 4, 2, SUB, PW), BF),
@@ -543,9 +554,12 @@
             vmem((NJ, 2, SUB, PW), BF),
             vmem((NJ, 2, 2, SUB, PW), BF),
             vmem((NJ, 2, SUB, PW), BF),
+            vmem((NJ, 2, SUB, PW), BF),
+            vmem((NJ, 32, CH), BF),
+            vmem((256, 160), BF),
             vmem((2, 160, TOK), BF),
-            vmem((2, TOK, TOK), BF),
-            vmem((2, TOK, TOK), F32),
+            vmem((2, 2, 8, TOK), jnp.int32),
+            vmem((2, 32, TOK), F32),
             vmem((256, 256), BF),
             vmem((256, 256), BF),
             vmem((ROWS, CH), BF),
@@ -560,13 +574,14 @@
             vmem((2, 8, FFD), F32),
             vmem((8, FFD), F32),
             vmem((8, FFD), F32),
-            vmem((TOK, 8), F32),
+            vmem((8, TOK), F32),
             pltpu.SemaphoreType.DMA((NK, NJ)),
             pltpu.SemaphoreType.DMA((NK, NJ)),
             pltpu.SemaphoreType.DMA((NX,)),
             pltpu.SemaphoreType.DMA((NX,)),
             pltpu.SemaphoreType.DMA((NJ + 9,)),
             pltpu.SemaphoreType.DMA,
+            pltpu.SemaphoreType.DMA((NJ,)),
         ],
         compiler_params=pltpu.CompilerParams(
             collective_id=0, has_side_effects=True, vmem_limit_bytes=62 * 2**20
@@ -575,58 +590,51 @@
     )(*args)
 
 
-def spread_kernel(ff, fb, wt, gg, next_ref, prev_ref, gg_ref, sel, lhs):
+def spread_kernel(uf, ub, wt, gg, next_ref, prev_ref, gg_ref, lhs):
     @pl.when(pl.program_id(0) == 0)
     def _():
         gg_ref[0] = gg[...]
-        o = iota((256, 160), 0)
-        v = iota((256, 160), 1)
-        slot = (v >> 3) + jnp.where(v >= 80, 6, 0)
-        sel[...] = onehot(((v & 7) == (o >> 5)) & ((o & 31) == slot))
         for p in range(2):
-            w = wt[p][:, 0:32]
+            w = wt[p].T
             hi = w.astype(BF)
             lhs[p, :, 0:32] = hi
             lhs[p, :, 32:64] = (w - hi.astype(F32)).astype(BF)
 
-    for p, (src, dst) in enumerate(((ff, next_ref), (fb, prev_ref))):
-        v = jnp.concatenate(
-            [src[0, h, :, c * FFD:(c + 1) * FFD] for h in range(2) for c in range(5)], axis=0
-        )
-        u = nn(sel[...], v).astype(BF)
-        row = jnp.concatenate([u[k * 32:(k + 1) * 32] for k in range(8)], axis=1)
-        both = jnp.concatenate([row, row], axis=0)
+    for p, (src, dst) in enumerate(((uf, next_ref), (ub, prev_ref))):
+        both = jnp.concatenate([src[0], src[0]], axis=0)
         dst[0] = nn(lhs[p], both).astype(BF)
 
 
-def dense(fin, wt, gg):
+def dense(u, wt, gg):
     return pl.pallas_call(
         spread_kernel,
         grid=(NC,),
         out_shape=(
             jax.ShapeDtypeStruct((1, TOK, D), BF),
             jax.ShapeDtypeStruct((1, TOK, D), BF),
-            jax.ShapeDtypeStruct((1, TOK, 8), F32),
+            jax.ShapeDtypeStruct((1, 8, TOK), F32),
         ),
         in_specs=[
-            pl.BlockSpec((1, 2, SUB, PW), lambda i: (i, 0, 0, 0)),
-            pl.BlockSpec((1, 2, SUB, PW), lambda i: (i + NC, 0, 0, 0)),
-            pl.BlockSpec((2, TOK, TOK), lambda i: (0, 0, 0)),
-            pl.BlockSpec((TOK, 8), lambda i: (0, 0)),
+            pl.BlockSpec((1, 32, CH), lambda i: (i, 0, 0)),
+            pl.BlockSpec((1, 32, CH), lambda i: (i + NC, 0, 0)),
+            pl.BlockSpec((2, 32, TOK), lambda i: (0, 0, 0)),
+            pl.BlockSpec((8, TOK), lambda i: (0, 0)),
         ],
         out_specs=(
             pl.BlockSpec((1, TOK, CH), lambda i: (0, 0, i)),
             pl.BlockSpec((1, TOK, CH), lambda i: (0, 0, i)),
-            pl.BlockSpec((1, TOK, 8), lambda i: (0, 0, 0)),
+            pl.BlockSpec((1, 8, TOK), lambda i: (0, 0, 0)),
         ),
-        scratch_shapes=[pltpu.VMEM((256, 160), BF), pltpu.VMEM((2, TOK, 64), BF)],
+        scratch_shapes=[pltpu.VMEM((2, TOK, 64), BF)],
         name="dense",
-    )(fin, fin, wt, gg)
+    )(u, u, wt, gg)
 
 
 def body(*args):
-    fin, wt, gg = relay(*args)
-    return dense(fin, wt, gg)
+    args = args[:2] + tuple(jnp.swapaxes(x, 1, 2) for x in args[2:6]) + args[6:]
+    u, wt, gg = relay(*args)
+    nxt, prv, grad = dense(u, wt, gg)
+    return nxt, prv, jnp.swapaxes(grad, 1, 2)
 
 
 def solution(mesh):

time: 152 us -> 132 us (0.87)
  Pallas kernels: 144 us -> 131 us
  local copies, waits for them, and re-layouts: 7.16 us -> 0 us
    pallas_call x1, Pallas kernels: 137 us -> 125 us  [relay(): pl.pallas_call(relay_kernel, out_shape=(jax.ShapeDtypeStruct((NJ, 32, CH)...]
    unnamed x4 -> x0, local copies, waits for them, and re-layouts: 5.66 us -> none
where the time goes in v2:
time: 132 us; the launch traced here: 131 us
  Pallas kernels  131 us (99%)
    pallas_call x1, Pallas kernels, relay(): pl.pallas_call(relay_kernel, out_shape=(jax.ShapeDtypeStruct((NJ, 32, CH)...  125 us
    pallas_call x1, Pallas kernels, dense(): pl.pallas_call(spread_kernel, grid=(NC,), out_shape=(jax.ShapeDtypeStruct...  5.95 us

profile of v2, /device:TPU:1, one launch (start us, length us, event | category | flops | bytes accessed | tf_op | source)
XLA Modules:
  0.0 131.2 jit_solution(12960347875312993172)
XLA Ops:
  0.6 124.6 %relay.1 = (bf16[14,32,1024]{2,1,0:T(8,128)(2,1)}, f32[2,32,128]{2,1,0:T(8,128)}, f32[8,128]{1,0:T(8,128)}) custom-call(bf16[1,128,7168]{2,1,0:T(8,128)(2,1)} %act.1, bf16[1,128,7168]{2,1,0:T(8,128)(2,1)} %cot.1, s32[1,8,128]{2,1,0:T(8,128)} %bitcast.5, f32[1,8,128]{2,1,0:T(8,128)} %bitcast.6, s32[1,8,128]{2,1,0:T(8,128)} %bitcast.7, f32[1,8,128]{2,1,0:T(8,128)} %bitcast.8, ...), custom_call_target="tpu_custom_call" | custom-call | tf_op jit(solution)/shard_map/relay/pallas_call | solution.py:532
  125.2 6.0 %dense.1 = (bf16[1,128,7168]{2,1,0:T(8,128)(2,1)}, bf16[1,128,7168]{2,1,0:T(8,128)(2,1)}, f32[1,8,128]{2,1,0:T(8,128)}) custom-call(bf16[14,32,1024]{2,1,0:T(8,128)(2,1)} %get-tuple-element.9.uf.ub, bf16[14,32,1024]{2,1,0:T(8,128)(2,1)} %get-tuple-element.9.uf.ub, f32[2,32,128]{2,1,0:T(8,128)} %get-tuple-element.10.wt, f32[8,128]{1,0:T(8,128)} %get-tuple-element.11.gg), custom_call_target="tpu_custom_call" | custom-call | tf_op jit(solution)/shard_map/dense/pallas_call | solution.py:609

commit v3 on v2

v3 whole, which is shorter than its diff:
```python
import jax
import jax.numpy as jnp
from jax import lax
from jax.experimental import pallas as pl
from jax.experimental.pallas import tpu as pltpu
from jax.sharding import PartitionSpec as P

MESH = pl.DeviceIdType.MESH
BF = jnp.bfloat16
F32 = jnp.float32

D = 7168
NC = 7
CH = D // NC
NJ = 2 * NC
TOK = 128
FFD = 128
SUB = 16
PW = 640
ROWS = 320

(Z, A_L, A_R, F_L, F_R, G_L, G_R, B_L, B_R, FB_L, FB_R) = range(11)
(BO_L, BO_R, BN_L, BN_R, AN_L, AN_R, AO_L, AO_R, AF_L, AF_R, FIN0, FIN1) = range(11, 23)
NK = 23
(DBO, DBN_L, DBN_R, DAO, DAN_L, DAN_R, DZ, WT0, WT1) = range(9)
(PX_G, PX_U, HID_L, HID_R, GH_L, GH_R, GG_G, GG_U) = range(9, 17)
NX = 17
(W_G, W_U, W_DL, W_DR) = range(4)

HF = CH // 2
CUT = 384

E1, E2, E3, E4, E5 = 1, 3, 5, 7, 9
X1 = E5 + NC + 1
X2 = X1 + 2
R0 = E5 + 11
X3 = E5 + NJ + 1
X4 = X3 + 2
R1, R2, R3, R4, R5 = R0 + 2, R0 + 4, R0 + 6, R0 + 8, R0 + 10
STEPS = NJ + R5


def iota(shape, dim):
    return lax.broadcasted_iota(jnp.int32, shape, dim)


def onehot(cond):
    return jnp.where(cond, 1.0, 0.0).astype(BF)


def nn(a, b):
    return jnp.dot(a, b, preferred_element_type=F32)


def nt(a, b):
    return lax.dot_general(a, b, (((1,), (1,)), ((), ())), preferred_element_type=F32)


def relay_kernel(
    act, cot, fids, fgates, bids, bgates, gw, uw, dw, gpre, upre,
    u_out, wt_out, gg_out,
    tok, gu, wd, ids, gates, pre, pref, obuf, zbuf, zin, sbuf, gbuf, fst0, fst1,
    qbuf, bo, bn, an, ao, afs0, afs1, fbuf, fin, ubuf, sel,
    lhs, rk, wts, perm_u, perm_p, xbuf, acc, accb, px, prx, hid, hx, hcat, ghx, ghr, gga, ggx, ggu,
    dbuf, dbo, dbn, dao, dan, dfin, dz, ggb,
    ssem, rsem, wss, wrs, xs, xr, lsem, wsem, osem, usem,
):
    sec = lax.axis_index("section")
    exp = lax.axis_index("expert")
    core = lax.rem(sec, 2)
    zlo = exp // 16
    cx = lax.rem(exp // 4, 4)
    cy = lax.rem(exp, 4)
    a = cx * (1 - core) + cy * core
    b = cy * (1 - core) + cx * core
    half = lax.rem(a, 2)
    al, ar, aopp = lax.rem(a + 3, 4), lax.rem(a + 1, 4), lax.rem(a + 2, 4)
    bl, br, bopp = lax.rem(b + 3, 4), lax.rem(b + 1, 4), lax.rem(b + 2, 4)

    def plane(ap, bp):
        return zlo * 16 + ap * (4 - 3 * core) + bp * (1 + 3 * core)

    partner = exp + 16 - 32 * zlo
    dev_al, dev_ar = {"expert": plane(al, b)}, {"expert": plane(ar, b)}
    dev_bl, dev_br = {"expert": plane(a, bl)}, {"expert": plane(a, br)}
    dev_p1 = {"expert": plane(a + 1 - 2 * half, b)}
    dev_p2 = {"expert": plane(lax.rem(a + 3 + 2 * half, 4), b)}
    dev_z = {"expert": partner}
    nxt, prv = lax.rem(sec + 1, 8), lax.rem(sec + 7, 8)

    def load(src, dst, k):
        return pltpu.make_async_copy(src, dst, lsem.at[k])

    small = [
        load(fids.at[0], ids.at[0], NJ),
        load(bids.at[0], ids.at[1], NJ + 1),
        load(fgates.at[0], gates.at[0], NJ + 2),
        load(bgates.at[0], gates.at[1], NJ + 3),
    ]
    pres = [
        load(gpre.at[0], pre.at[:, pl.ds(0, FFD)], NJ + 4),
        load(upre.at[0], pre.at[:, pl.ds(FFD, FFD)], NJ + 5),
    ]
    toks = []
    for j in range(NJ):
        src = act if j < NC else cot
        toks.append(load(src.at[0, :, pl.ds((j % NC) * CH, CH)], tok.at[j], j))

    def feats(i, h):
        return pl.ds(pl.multiple_of(i * CH + h * HF, HF), HF)

    def own_weight(k, i):
        src = (gw, uw, dw)[k]
        if k < 2:
            src = src.at[0, feats(i, half), :]
            dst = gu.at[i, :, pl.ds(2 * k * FFD, FFD)]
        else:
            src = src.at[0, :, feats(i, half)]
            dst = wd.at[i, pl.ds(0, FFD), :]
        return pltpu.make_async_copy(src, dst, wsem.at[k, i])

    for c in small:
        c.start()
    for c in toks[:NC]:
        c.start()
    for i in range(NC):
        own_weight(0, i).start()
        own_weight(1, i).start()
    for c in toks[NC:]:
        c.start()
    for i in range(NC):
        own_weight(2, i).start()
    for c in pres:
        c.start()

    barrier = pltpu.get_barrier_semaphore()
    peers = [dev_al, dev_ar, dev_bl, dev_br, dev_z]
    for s in (nxt, prv):
        peers.append({"section": s, "expert": exp})
        peers.append({"section": s, "expert": partner})
    for dev in peers:
        pl.semaphore_signal(barrier, inc=1, device_id=dev, device_id_type=MESH)

    for c in small:
        c.wait()
    upper = onehot(iota((TOK, TOK), 0) <= iota((TOK, TOK), 1))
    slot16 = iota((16, TOK), 0)
    row160 = iota((160, TOK), 0)
    row_slot = (jnp.where(row160 >= 80, row160 - 80, row160) >> 4) * 2 + ((row160 >> 2) & 1)
    for p in range(2):
        ranks = []
        for h in range(2):
            e = zlo if h == 0 else 1 - zlo
            match = ids[p] == e
            routed = jnp.max(jnp.where(match, 1.0, 0.0), axis=0, keepdims=True)
            w = jnp.sum(jnp.where(match, gates[p], 0.0), axis=0, keepdims=True)
            count = nn(jnp.broadcast_to(routed, (8, TOK)).astype(BF), upper)
            rank = jnp.where(routed > 0.5, count.astype(jnp.int32) - 1, -1)
            rk[p, h] = rank
            wts[p, h * 16:h * 16 + 16] = jnp.where(slot16 == rank[0:1], w, 0.0)
            ranks.append(rank[0:1])
        low = jnp.where(row_slot == ranks[0], 1.0, 0.0)
        high = jnp.where(row_slot == ranks[1], 1.0, 0.0)
        lhs[p] = jnp.where(row160 < 80, low, high).astype(BF)
    pl.semaphore_wait(barrier, len(peers))

    def extra(src, dst, k, dev):
        return pltpu.make_async_remote_copy(
            src_ref=src, dst_ref=dst, send_sem=xs.at[k], recv_sem=xr.at[k],
            device_id=dev, device_id_type=MESH,
        )

    wt_copies = [
        extra(wts.at[0], wt_out.at[0], WT0, {"section": nxt, "expert": exp}),
        extra(wts.at[1], wt_out.at[1], WT1, {"section": prv, "expert": exp}),
    ]
    for c in wt_copies:
        c.start()

    def weight(k, i):
        other = 1 - half
        if k == W_G:
            src, dst, dev = gw.at[0, feats(i, other), :], gu.at[i, :, pl.ds(FFD, FFD)], dev_p1
        elif k == W_U:
            src, dst, dev = uw.at[0, feats(i, other), :], gu.at[i, :, pl.ds(3 * FFD, FFD)], dev_p2
        elif k == W_DL:
            src = dw.at[0, pl.ds(64, 64), feats(i, other)]
            dst, dev = wd.at[i, pl.ds(192, 64), :], dev_ar
        else:
            src = dw.at[0, pl.ds(0, 64), feats(i, other)]
            dst, dev = wd.at[i, pl.ds(128, 64), :], dev_al
        return pltpu.make_async_remote_copy(
            src_ref=src, dst_ref=dst, send_sem=wss.at[k, i], recv_sem=wrs.at[k, i],
            device_id=dev, device_id_type=MESH,
        )

    def ring(src, dst, k, j, dev):
        return pltpu.make_async_remote_copy(
            src_ref=src, dst_ref=dst, send_sem=ssem.at[k, j], recv_sem=rsem.at[k, j],
            device_id=dev, device_id_type=MESH,
        )

    lo, hi = pl.ds(0, CUT), pl.ds(CUT, PW - CUT)

    def out(k, j):
        if k == Z:
            return ring(zbuf.at[j], zin.at[j], k, j, dev_z)
        if k == A_L:
            return ring(sbuf.at[j], gbuf.at[j, b, a], k, j, dev_ar)
        if k == A_R:
            return ring(sbuf.at[j], gbuf.at[j, b, a], k, j, dev_al)
        if k == F_L:
            return ring(gbuf.at[j, b, a, :, lo], fst0.at[j], k, j, dev_ar)
        if k == F_R:
            return ring(gbuf.at[j, b, a, :, hi], fst1.at[j], k, j, dev_al)
        if k == G_L:
            return ring(fst0.at[j], gbuf.at[j, b, al, :, lo], k, j, dev_ar)
        if k == G_R:
            return ring(fst1.at[j], gbuf.at[j, b, ar, :, hi], k, j, dev_al)
        if k == B_L:
            return ring(gbuf.at[j, b], gbuf.at[j, b], k, j, dev_br)
        if k == B_R:
            return ring(gbuf.at[j, b], gbuf.at[j, b], k, j, dev_bl)
        if k == FB_L:
            two = gbuf.at[j, bl, pl.ds(0, 2)]
            return ring(two, two, k, j, dev_br)
        if k == FB_R:
            two = gbuf.at[j, br, pl.ds(2, 2)]
            return ring(two, two, k, j, dev_bl)
        if k == BO_L:
            return ring(qbuf.at[j, bopp, pl.ds(0, 2)], bo.at[j, 0], k, j, dev_br)
        if k == BO_R:
            return ring(qbuf.at[j, bopp, pl.ds(2, 2)], bo.at[j, 1], k, j, dev_bl)
        if k == BN_L:
            return ring(qbuf.at[j, br], bn.at[j, 0], k, j, dev_br)
        if k == BN_R:
            return ring(qbuf.at[j, bl], bn.at[j, 1], k, j, dev_bl)
        if k == AN_L:
            return ring(qbuf.at[j, b, ar], an.at[j, 0], k, j, dev_ar)
        if k == AN_R:
            return ring(qbuf.at[j, b, al], an.at[j, 1], k, j, dev_al)
        if k == AO_L:
            return ring(qbuf.at[j, b, aopp, :, lo], afs0.at[j], k, j, dev_ar)
        if k == AO_R:
            return ring(qbuf.at[j, b, aopp, :, hi], afs1.at[j], k, j, dev_al)
        if k == AF_L:
            return ring(afs0.at[j], ao.at[j, :, lo], k, j, dev_ar)
        if k == AF_R:
            return ring(afs1.at[j], ao.at[j, :, hi], k, j, dev_al)
        to = jnp.where(j < NC, nxt, prv)
        h = k - FIN0
        dev = {"section": to, "expert": exp if h == 0 else partner}
        return ring(fbuf.at[j, h], fin.at[j, h], k, j, dev)

    def arrived(k, j):
        dst = {
            Z: lambda: zin.at[j],
            A_L: lambda: gbuf.at[j, b, al],
            A_R: lambda: gbuf.at[j, b, ar],
            F_L: lambda: fst0.at[j],
            F_R: lambda: fst1.at[j],
            G_L: lambda: gbuf.at[j, b, aopp, :, lo],
            G_R: lambda: gbuf.at[j, b, aopp, :, hi],
            B_L: lambda: gbuf.at[j, bl],
            B_R: lambda: gbuf.at[j, br],
            FB_L: lambda: gbuf.at[j, bopp, pl.ds(0, 2)],
            FB_R: lambda: gbuf.at[j, bopp, pl.ds(2, 2)],
            BO_L: lambda: bo.at[j, 0],
            BO_R: lambda: bo.at[j, 1],
            BN_L: lambda: bn.at[j, 0],
            BN_R: lambda: bn.at[j, 1],
            AN_L: lambda: an.at[j, 0],
            AN_R: lambda: an.at[j, 1],
            AO_L: lambda: afs0.at[j],
            AO_R: lambda: afs1.at[j],
            AF_L: lambda: ao.at[j, :, lo],
            AF_R: lambda: ao.at[j, :, hi],
            FIN0: lambda: fin.at[j, 0],
            FIN1: lambda: fin.at[j, 1],
        }[k]()
        ring(dst, dst, k, j, dev_z).wait_recv()

    def send(*kinds, j):
        for k in kinds:
            out(k, j).start()

    def sent(*kinds, j):
        for k in kinds:
            out(k, j).wait_send()

    def f32(v):
        return v.astype(F32)

    r16 = iota((SUB, FFD), 0)
    row_k = ((r16 >> 3) << 2) | (r16 & 3)

    def pack(j):
        p = j // NC
        load(act.at[0, :, pl.ds(0, CH)], tok.at[j], j).wait()
        y = nn(lhs[p], tok[j])
        for h in range(2):
            for c in range(5):
                r = (h * 5 + c) * SUB
                v = y[r:r + SUB, 0:FFD]
                for k in range(1, 8):
                    v = jnp.where(row_k == k, y[r:r + SUB, k * FFD:(k + 1) * FFD], v)
                if h == 0:
                    obuf[j, :, c * FFD:(c + 1) * FFD] = v.astype(BF)
                else:
                    zbuf[j, :, c * FFD:(c + 1) * FFD] = v.astype(BF)

    def by_half(j):
        o, z = f32(obuf[j]), f32(zin[j])
        first = jnp.concatenate([o[0:8], z[0:8]], axis=0)
        second = jnp.concatenate([o[8:16], z[8:16]], axis=0)
        gbuf[j, b, a] = jnp.where(half == 0, first, second).astype(BF)
        sbuf[j] = jnp.where(half == 0, second, first).astype(BF)

    def tables():
        o = iota((256, 256), 0)
        i = iota((256, 256), 1)
        perm_u[...] = onehot(i == ((o & 63) >> 2) * 16 + (o & 3) * 4 + (o >> 6))
        perm_p[...] = onehot(o == ((i & 63) >> 2) * 16 + (i & 3) * 4 + (i >> 6))
        o = iota((256, 160), 0)
        v = iota((256, 160), 1)
        h = jnp.where(v >= 80, 1, 0)
        slot = h * 16 + ((v - 80 * h) >> 4) * 2 + ((v >> 2) & 1)
        k = (((v >> 3) & 1) << 2) | (v & 3)
        sel[...] = onehot((k == (o >> 5)) & ((o & 31) == slot))

    def saved():
        for c in pres:
            c.wait()
        i = iota((ROWS, ROWS), 0)
        h = (i >> 1) & 1
        bp = (i >> 4) & 3
        ap = (i >> 2) & 3
        xy = ap * (4 - 3 * core) + bp * (1 + 3 * core)
        pln = zlo + h - 2 * zlo * h
        src = (pln * 16 + xy) * 10 + (i >> 6) * 2 + (i & 1)
        pref[...] = nn(onehot(iota((ROWS, ROWS), 1) == src), pre[...])

    def unpack(j):
        r = nn(perm_u[...], gbuf[j].reshape(256, PW)).astype(BF)
        for c in range(5):
            for k in range(4):
                xbuf[c * 64:(c + 1) * 64, k * FFD:(k + 1) * FFD] = (
                    r[k * 64:(k + 1) * 64, c * FFD:(c + 1) * FFD]
                )

    def repack(j, o):
        o = o.astype(BF)
        cols = []
        for c in range(5):
            cols.append(
                jnp.concatenate(
                    [o[c * 64:(c + 1) * 64, k * FFD:(k + 1) * FFD] for k in range(4)], axis=0
                )
            )
        q = nn(perm_p[...], jnp.concatenate(cols, axis=1)).astype(BF)
        qbuf[j] = q.reshape(4, 4, SUB, PW)

    def px_copies():
        return [
            extra(px.at[0], prx.at[0], PX_G, dev_p1),
            extra(px.at[1], prx.at[1], PX_U, dev_p2),
        ]

    def hid_copies():
        return [
            extra(hid, hx.at[0], HID_L, dev_ar),
            extra(hid, hx.at[1], HID_R, dev_al),
        ]

    def gh_copies():
        return [
            extra(ghx, ghr.at[0], GH_L, dev_ar),
            extra(ghx, ghr.at[1], GH_R, dev_al),
        ]

    def gg_copies():
        return [
            extra(gga.at[0], ggx.at[0], GG_G, dev_p1),
            extra(gga.at[1], ggx.at[1], GG_U, dev_p2),
        ]

    def forward_rows(i):
        own_weight(0, i).wait()
        own_weight(1, i).wait()
        weight(W_G, i).wait()
        weight(W_U, i).wait()

        @pl.when(i == 0)
        def _():
            acc[...] = nn(xbuf[...], gu[i])

        @pl.when(i > 0)
        def _():
            acc[...] += nn(xbuf[...], gu[i])

        @pl.when(i == NC - 1)
        def _():
            px[0] = acc[:, FFD:2 * FFD].astype(BF)
            px[1] = acc[:, 3 * FFD:4 * FFD].astype(BF)
            for c in px_copies():
                c.start()

    def backward_rows(i):
        own_weight(2, i).wait()
        weight(W_DL, i).wait()
        weight(W_DR, i).wait()

        @pl.when(i == 0)
        def _():
            accb[...] = nt(xbuf[...], wd[i])

        @pl.when(i > 0)
        def _():
            accb[...] += nt(xbuf[...], wd[i])

        @pl.when(i == NC - 1)
        def _():
            ghx[...] = accb[:, FFD:2 * FFD].astype(BF)
            for c in gh_copies():
                c.start()

    left64 = iota((ROWS, FFD), 1) < 64

    def hidden_own():
        for c in px_copies():
            c.wait()
        g = acc[:, 0:FFD] + f32(prx[0])
        u = acc[:, 2 * FFD:3 * FFD] + f32(prx[1])
        hid[...] = (g / (1.0 + jnp.exp(-g)) * u).astype(BF)
        for c in hid_copies():
            c.start()

    def hidden_all():
        for c in hid_copies():
            c.wait()
        hcat[:, 0:FFD] = hid[...]
        hcat[:, FFD:2 * FFD] = jnp.where(left64, f32(hx[1]), f32(hx[0])).astype(BF)

    def grads_own():
        for c in gh_copies():
            c.wait()
        gh = accb[:, 0:FFD] + jnp.where(left64, f32(ghr[0]), f32(ghr[1]))
        g = pref[:, 0:FFD]
        u = pref[:, FFD:2 * FFD]
        s = 1.0 / (1.0 + jnp.exp(-g))
        silu = g * s
        gga[0] = (gh * u * s * (1.0 + g * (1.0 - s))).astype(BF)
        gga[1] = (gh * silu).astype(BF)
        for c in gg_copies():
            c.start()
        dots = jnp.sum(gh * silu * u, axis=1, keepdims=True)
        at = iota((ROWS, FFD), 1) == (iota((ROWS, FFD), 0) >> 6)
        spot = jnp.where(at, jnp.broadcast_to(dots, (ROWS, FFD)), 0.0).astype(BF)
        o = iota((FFD, ROWS), 0)
        i2 = iota((FFD, ROWS), 1) & 63
        pick = onehot(((o & 7) < 4) & (i2 == (o >> 3) * 4 + (o & 7)))
        dbuf[...] = nn(pick, spot).reshape(4, 4, 8, FFD)

    def grads_all():
        for c in gg_copies():
            c.wait()
        ggu[:, 0:FFD] = gga[0]
        ggu[:, FFD:2 * FFD] = ggx[0]
        ggu[:, 2 * FFD:3 * FFD] = gga[1]
        ggu[:, 3 * FFD:4 * FFD] = ggx[1]

    @pl.loop(0, STEPS)
    def _(t):
        def event(lag, lo=0, hi=NJ):
            def wrap(f):
                @pl.when((t - lag >= lo) & (t - lag < hi))
                def _():
                    f(t - lag)
            return wrap

        @event(0)
        def _(j):
            pack(j)
            send(Z, j=j)

            @pl.when(j == 1)
            def _():
                tables()

        @event(E1)
        def _(j):
            arrived(Z, j)
            by_half(j)
            send(A_L, A_R, F_L, F_R, j=j)

            @pl.when(j < NC)
            def _():
                weight(W_G, j).start()
                weight(W_U, j).start()

            @pl.when(j >= NC)
            def _():
                weight(W_DL, j - NC).start()
                weight(W_DR, j - NC).start()

        @event(E2)
        def _(j):
            arrived(F_L, j)
            send(G_L, j=j)
            arrived(F_R, j)
            send(G_R, j=j)

        @event(E3)
        def _(j):
            arrived(A_L, j)
            arrived(A_R, j)
            arrived(G_L, j)
            arrived(G_R, j)
            send(B_L, B_R, j=j)

        @event(E4)
        def _(j):
            arrived(B_L, j)
            send(FB_L, j=j)
            arrived(B_R, j)
            send(FB_R, j=j)

        for step, act_now in ((X1, hidden_own), (X2, hidden_all), (X3, grads_own), (X4, grads_all)):
            pl.when(t == step)(act_now)

        @event(R0)
        def _(j):
            @pl.when(j < NC)
            def _():
                repack(j, nn(hcat[...], wd[j]))

            @pl.when(j >= NC)
            def _():
                repack(j, nt(ggu[...], gu[j - NC]))

            send(BO_L, BO_R, j=j)

            @pl.when(j == NC)
            def _():
                extra(dbuf.at[bopp], dbo, DBO, dev_br).start()

        @event(R1)
        def _(j):
            arrived(BO_L, j)
            qbuf[j, br, 0:2] = (f32(qbuf[j, br, 0:2]) + f32(bo[j, 0])).astype(BF)
            send(BN_L, j=j)
            arrived(BO_R, j)
            qbuf[j, bl, 2:4] = (f32(qbuf[j, bl, 2:4]) + f32(bo[j, 1])).astype(BF)
            send(BN_R, j=j)

            @pl.when(j == NC)
            def _():
                extra(dbuf.at[bopp], dbo, DBO, dev_br).wait()
                dbuf[br] = dbuf[br] + dbo[...]
                extra(dbuf.at[br], dbn.at[0], DBN_L, dev_br).start()
                extra(dbuf.at[bl], dbn.at[1], DBN_R, dev_bl).start()

        @event(R2)
        def _(j):
            arrived(BN_L, j)
            arrived(BN_R, j)
            qbuf[j, b] = (f32(qbuf[j, b]) + f32(bn[j, 0]) + f32(bn[j, 1])).astype(BF)
            send(AO_L, AO_R, AN_L, AN_R, j=j)

            @pl.when(j == NC)
            def _():
                extra(dbuf.at[br], dbn.at[0], DBN_L, dev_br).wait()
                extra(dbuf.at[bl], dbn.at[1], DBN_R, dev_bl).wait()
                dbuf[b] = dbuf[b] + dbn[0] + dbn[1]
                extra(dbuf.at[b, aopp], dao, DAO, dev_ar).start()

        @event(R3)
        def _(j):
            arrived(AO_L, j)
            send(AF_L, j=j)
            arrived(AO_R, j)
            send(AF_R, j=j)

            @pl.when(j == NC)
            def _():
                extra(dbuf.at[b, aopp], dao, DAO, dev_ar).wait()
                dbuf[b, ar] = dbuf[b, ar] + dao[...]
                extra(dbuf.at[b, ar], dan.at[0], DAN_L, dev_ar).start()
                extra(dbuf.at[b, al], dan.at[1], DAN_R, dev_al).start()

        @event(R4)
        def _(j):
            arrived(AN_L, j)
            arrived(AN_R, j)
            arrived(AF_L, j)
            arrived(AF_R, j)
            mine = f32(qbuf[j, b, a]) + f32(ao[j])
            theirs = f32(an[j, 0]) + f32(an[j, 1])
            first = jnp.where(half == 0, mine, theirs)
            second = jnp.where(half == 0, theirs, mine)
            for h in range(2):
                r = h * 8
                fbuf[j, h] = jnp.concatenate([first[r:r + 8], second[r:r + 8]], axis=0).astype(BF)
            send(FIN0, FIN1, j=j)

            @pl.when(j == NC)
            def _():
                extra(dbuf.at[b, ar], dan.at[0], DAN_L, dev_ar).wait()
                extra(dbuf.at[b, al], dan.at[1], DAN_R, dev_al).wait()
                dfin[...] = dbuf[b, a] + dan[0] + dan[1]
                extra(dfin, dz, DZ, dev_z).start()

        @event(R5)
        def _(j):
            arrived(FIN0, j)
            arrived(FIN1, j)
            v = jnp.concatenate(
                [fin[j, h, :, c * FFD:(c + 1) * FFD] for h in range(2) for c in range(5)], axis=0
            )
            u = nn(sel[...], v).astype(BF)
            for k in range(8):
                ubuf[j, :, k * FFD:(k + 1) * FFD] = u[k * 32:(k + 1) * 32]
            pltpu.make_async_copy(ubuf.at[j], u_out.at[j], usem.at[j]).start()
            sent(
                BO_L, BO_R, BN_L, BN_R, AN_L, AN_R, AO_L, AO_R, AF_L, AF_R, FIN0, FIN1, j=j
            )

            @pl.when(j == NC)
            def _():
                extra(dfin, dz, DZ, dev_z).wait()
                la = iota((8, FFD), 0)
                mine = jnp.where(la < 2, dfin[...], dz[...]).T
                c8 = iota((8, TOK), 0)
                which = ids[1]
                total = jnp.zeros((8, TOK), F32)
                for h in range(2):
                    d = jnp.zeros((8, TOK), F32)
                    for par in range(2):
                        hit = jnp.where((rk[1, h, 0:1] == c8 * 2 + par) & (c8 < 5), 1.0, 0.0)
                        d = d + hit * mine[0:8, h * 2 + par:h * 2 + par + 1]
                    d = jnp.sum(d, axis=0, keepdims=True)
                    e = zlo if h == 0 else 1 - zlo
                    total = total + jnp.where(which == e, d, 0.0)
                ggb[...] = total
                pltpu.make_async_copy(ggb, gg_out, osem).start()

        @event(E5)
        def _(j):
            @pl.when(j == 0)
            def _():
                saved()

            arrived(FB_L, j)
            arrived(FB_R, j)
            unpack(j)

            @pl.when(j < NC)
            def _():
                forward_rows(j)

            @pl.when(j >= NC)
            def _():
                backward_rows(j - NC)

            sent(Z, A_L, A_R, F_L, F_R, G_L, G_R, B_L, B_R, FB_L, FB_R, j=j)

    for c in wt_copies:
        c.wait()
    pltpu.make_async_copy(ggb, gg_out, osem).wait()
    for j in range(NJ):
        pltpu.make_async_copy(ubuf.at[j], u_out.at[j], usem.at[j]).wait()


def relay(*args):
    any_spec = pl.BlockSpec(memory_space=pl.ANY)
    vmem = pltpu.VMEM
    dma = pltpu.SemaphoreType.DMA
    return pl.pallas_call(
        relay_kernel,
        out_shape=(
            jax.ShapeDtypeStruct((NJ, 32, CH), BF),
            jax.ShapeDtypeStruct((2, 32, TOK), F32),
            jax.ShapeDtypeStruct((8, TOK), F32),
        ),
        in_specs=[any_spec] * 11,
        out_specs=(any_spec,) * 3,
        scratch_shapes=[
            vmem((NJ, TOK, CH), BF),
            vmem((NC, HF, 4 * FFD), BF),
            vmem((NC, 2 * FFD, HF), BF),
            vmem((2, 8, TOK), jnp.int32),
            vmem((2, 8, TOK), F32),
            vmem((ROWS, 2 * FFD), BF),
            vmem((ROWS, 2 * FFD), F32),
            vmem((NJ, SUB, PW), BF),
            vmem((NJ, SUB, PW), BF),
            vmem((NJ, SUB, PW), BF),
            vmem((NJ, SUB, PW), BF),
            vmem((NJ, 4, 4, SUB, PW), BF),
            vmem((NJ, SUB, CUT), BF),
            vmem((NJ, SUB, PW - CUT), BF),
            vmem((NJ, 4, 4, SUB, PW), BF),
            vmem((NJ, 2, 2, SUB, PW), BF),
            vmem((NJ, 2, 4, SUB, PW), BF),
            vmem((NJ, 2, SUB, PW), BF),
            vmem((NJ, SUB, PW), BF),
            vmem((NJ, SUB, CUT), BF),
            vmem((NJ, SUB, PW - CUT), BF),
            vmem((NJ, 2, SUB, PW), BF),
            vmem((NJ, 2, SUB, PW), BF),
            vmem((NJ, 32, CH), BF),
            vmem((256, 160), BF),
            vmem((2, 160, TOK), BF),
            vmem((2, 2, 8, TOK), jnp.int32),
            vmem((2, 32, TOK), F32),
            vmem((256, 256), BF),
            vmem((256, 256), BF),
            vmem((ROWS, HF), BF),
            vmem((ROWS, 4 * FFD), F32),
            vmem((ROWS, 2 * FFD), F32),
            vmem((2, ROWS, FFD), BF),
            vmem((2, ROWS, FFD), BF),
            vmem((ROWS, FFD), BF),
            vmem((2, ROWS, FFD), BF),
            vmem((ROWS, 2 * FFD), BF),
            vmem((ROWS, FFD), BF),
            vmem((2, ROWS, FFD), BF),
            vmem((2, ROWS, FFD), BF),
            vmem((2, ROWS, FFD), BF),
            vmem((ROWS, 4 * FFD), BF),
            vmem((4, 4, 8, FFD), F32),
            vmem((4, 8, FFD), F32),
            vmem((2, 4, 8, FFD), F32),
            vmem((8, FFD), F32),
            vmem((2, 8, FFD), F32),
            vmem((8, FFD), F32),
            vmem((8, FFD), F32),
            vmem((8, TOK), F32),
            dma((NK, NJ)),
            dma((NK, NJ)),
            dma((4, NC)),
            dma((4, NC)),
            dma((NX,)),
            dma((NX,)),
            dma((NJ + 6,)),
            dma((3, NC)),
            dma,
            dma((NJ,)),
        ],
        compiler_params=pltpu.CompilerParams(
            collective_id=0, has_side_effects=True, vmem_limit_bytes=62 * 2**20
        ),
        name="relay",
    )(*args)


def spread_kernel(uf, ub, wt, gg, next_ref, prev_ref, gg_ref, lhs):
    @pl.when(pl.program_id(0) == 0)
    def _():
        gg_ref[0] = gg[...]
        for p in range(2):
            w = wt[p].T
            hi = w.astype(BF)
            lhs[p, :, 0:32] = hi
            lhs[p, :, 32:64] = (w - hi.astype(F32)).astype(BF)

    for p, (src, dst) in enumerate(((uf, next_ref), (ub, prev_ref))):
        both = jnp.concatenate([src[0], src[0]], axis=0)
        dst[0] = nn(lhs[p], both).astype(BF)


def dense(u, wt, gg):
    return pl.pallas_call(
        spread_kernel,
        grid=(NC,),
        out_shape=(
            jax.ShapeDtypeStruct((1, TOK, D), BF),
            jax.ShapeDtypeStruct((1, TOK, D), BF),
            jax.ShapeDtypeStruct((1, 8, TOK), F32),
        ),
        in_specs=[
            pl.BlockSpec((1, 32, CH), lambda i: (i, 0, 0)),
            pl.BlockSpec((1, 32, CH), lambda i: (i + NC, 0, 0)),
            pl.BlockSpec((2, 32, TOK), lambda i: (0, 0, 0)),
            pl.BlockSpec((8, TOK), lambda i: (0, 0)),
        ],
        out_specs=(
            pl.BlockSpec((1, TOK, CH), lambda i: (0, 0, i)),
            pl.BlockSpec((1, TOK, CH), lambda i: (0, 0, i)),
            pl.BlockSpec((1, 8, TOK), lambda i: (0, 0, 0)),
        ),
        scratch_shapes=[pltpu.VMEM((2, TOK, 64), BF)],
        name="dense",
    )(u, u, wt, gg)


def body(*args):
    args = args[:2] + tuple(jnp.swapaxes(x, 1, 2) for x in args[2:6]) + args[6:]
    u, wt, gg = relay(*args)
    nxt, prv, grad = dense(u, wt, gg)
    return nxt, prv, jnp.swapaxes(grad, 1, 2)


def solution(mesh):
    rows = P("section", "expert", None)
    cols = P("section", None, "expert")
    return jax.shard_map(
        body,
        mesh=mesh,
        in_specs=(rows,) * 6 + (cols, cols, rows, cols, cols),
        out_specs=(rows,) * 3,
        check_vma=False,
    )
```

time: 132 us -> 121 us (0.917)
  Pallas kernels: 131 us -> 120 us
    pallas_call x1, Pallas kernels: 125 us -> 114 us  [relay(): pl.pallas_call(relay_kernel, out_shape=(jax.ShapeDtypeStruct((NJ, 32, CH)...]
where the time goes in v3:
time: 121 us
  Pallas kernels  120 us (99%)
    pallas_call x1, Pallas kernels, relay(): pl.pallas_call(relay_kernel, out_shape=(jax.ShapeDtypeStruct((NJ, 32, CH)...  114 us
    pallas_call x1, Pallas kernels, dense(): pl.pallas_call(spread_kernel, grid=(NC,), out_shape=(jax.ShapeDtypeStruct...  5.96 us

profile of v3, /device:TPU:1, one launch (start us, length us, event | category | flops | bytes accessed | tf_op | source)
XLA Modules:
  0.0 120.9 jit_solution(11022774555852602524)
XLA Ops:
  0.6 114.3 %relay.1 = (bf16[14,32,1024]{2,1,0:T(8,128)(2,1)}, f32[2,32,128]{2,1,0:T(8,128)}, f32[8,128]{1,0:T(8,128)}) custom-call(bf16[1,128,7168]{2,1,0:T(8,128)(2,1)} %act.1, bf16[1,128,7168]{2,1,0:T(8,128)(2,1)} %cot.1, s32[1,8,128]{2,1,0:T(8,128)} %bitcast.5, f32[1,8,128]{2,1,0:T(8,128)} %bitcast.6, s32[1,8,128]{2,1,0:T(8,128)} %bitcast.7, f32[1,8,128]{2,1,0:T(8,128)} %bitcast.8, ...), custom_call_target="tpu_custom_call" | custom-call | tf_op jit(solution)/shard_map/relay/pallas_call | solution.py:678
  114.9 6.0 %dense.1 = (bf16[1,128,7168]{2,1,0:T(8,128)(2,1)}, bf16[1,128,7168]{2,1,0:T(8,128)(2,1)}, f32[1,8,128]{2,1,0:T(8,128)}) custom-call(bf16[14,32,1024]{2,1,0:T(8,128)(2,1)} %get-tuple-element.9.uf.ub, bf16[14,32,1024]{2,1,0:T(8,128)(2,1)} %get-tuple-element.9.uf.ub, f32[2,32,128]{2,1,0:T(8,128)} %get-tuple-element.10.wt, f32[8,128]{1,0:T(8,128)} %get-tuple-element.11.gg), custom_call_target="tpu_custom_call" | custom-call | tf_op jit(solution)/shard_map/dense/pallas_call | solution.py:773

commit v4 on v3

--- a/solution.py
+++ b/solution.py
@@ -19,25 +19,29 @@
 PW = 640
 ROWS = 320
 
-(Z, A_L, A_R, F_L, F_R, G_L, G_R, B_L, B_R, FB_L, FB_R) = range(11)
-(BO_L, BO_R, BN_L, BN_R, AN_L, AN_R, AO_L, AO_R, AF_L, AF_R, FIN0, FIN1) = range(11, 23)
-NK = 23
+(Z, A_L, A_R, A_O, B_L, B_R, FB_L, FB_R) = range(8)
+(BO_L, BO_R, BN_L, BN_R, AN_L, AN_R, AN_O, FIN0, FIN1) = range(8, 17)
+(GZ, GA, GB, GFB, GBO, GBN, GAN, GFIN) = range(8)
+NG = 8
+GROUP = (GZ, GA, GA, GA, GB, GB, GFB, GFB, GBO, GBO, GBN, GBN, GAN, GAN, GAN, GFIN, GFIN)
+BLOCKS = (1, 3, 8, 4, 4, 8, 3, 2)
+SENT = (16, 17)
 (DBO, DBN_L, DBN_R, DAO, DAN_L, DAN_R, DZ, WT0, WT1) = range(9)
 (PX_G, PX_U, HID_L, HID_R, GH_L, GH_R, GG_G, GG_U) = range(9, 17)
 NX = 17
 (W_G, W_U, W_DL, W_DR) = range(4)
 
+AHEAD = 2
 HF = CH // 2
-CUT = 384
-
-E1, E2, E3, E4, E5 = 1, 3, 5, 7, 9
-X1 = E5 + NC + 1
+
+E1, E2, E3, E4 = 1, 3, 5, 7
+X1 = E4 + NC + 1
 X2 = X1 + 2
-R0 = E5 + 11
-X3 = E5 + NJ + 1
+R0 = E4 + 11
+X3 = E4 + NJ + 1
 X4 = X3 + 2
-R1, R2, R3, R4, R5 = R0 + 2, R0 + 4, R0 + 6, R0 + 8, R0 + 10
-STEPS = NJ + R5
+R1, R2, R3, R4 = R0 + 2, R0 + 5, R0 + 8, R0 + 11
+STEPS = NJ + R4
 
 
 def iota(shape, dim):
@@ -59,10 +63,10 @@
 def relay_kernel(
     act, cot, fids, fgates, bids, bgates, gw, uw, dw, gpre, upre,
     u_out, wt_out, gg_out,
-    tok, gu, wd, ids, gates, pre, pref, obuf, zbuf, zin, sbuf, gbuf, fst0, fst1,
-    qbuf, bo, bn, an, ao, afs0, afs1, fbuf, fin, ubuf, sel,
+    tok, gu, wd, ids, gates, pre, pref, obuf, zbuf, zin, sbuf, gbuf,
+    qbuf, bo, bn, an, ao, fbuf, fin, ubuf, sel,
     lhs, rk, wts, perm_u, perm_p, xbuf, acc, accb, px, prx, hid, hx, hcat, ghx, ghr, gga, ggx, ggu,
-    dbuf, dbo, dbn, dao, dan, dfin, dz, ggb,
+    dbuf, dbo, dbn, dao, dan, dfin, dz, ggb, size,
     ssem, rsem, wss, wrs, xs, xr, lsem, wsem, osem, usem,
 ):
     sec = lax.axis_index("section")
@@ -82,6 +86,7 @@
 
     partner = exp + 16 - 32 * zlo
     dev_al, dev_ar = {"expert": plane(al, b)}, {"expert": plane(ar, b)}
+    dev_ao = {"expert": plane(aopp, b)}
     dev_bl, dev_br = {"expert": plane(a, bl)}, {"expert": plane(a, br)}
     dev_p1 = {"expert": plane(a + 1 - 2 * half, b)}
     dev_p2 = {"expert": plane(lax.rem(a + 3 + 2 * half, 4), b)}
@@ -134,7 +139,7 @@
         c.start()
 
     barrier = pltpu.get_barrier_semaphore()
-    peers = [dev_al, dev_ar, dev_bl, dev_br, dev_z]
+    peers = [dev_al, dev_ar, dev_ao, dev_bl, dev_br, dev_z]
     for s in (nxt, prv):
         peers.append({"section": s, "expert": exp})
         peers.append({"section": s, "expert": partner})
@@ -194,13 +199,16 @@
             device_id=dev, device_id_type=MESH,
         )
 
+    for i in range(AHEAD):
+        weight(W_G, i).start()
+        weight(W_U, i).start()
+
     def ring(src, dst, k, j, dev):
         return pltpu.make_async_remote_copy(
-            src_ref=src, dst_ref=dst, send_sem=ssem.at[k, j], recv_sem=rsem.at[k, j],
+            src_ref=src, dst_ref=dst,
+            send_sem=ssem.at[0 if k < BO_L else 1, j], recv_sem=rsem.at[GROUP[k], j],
             device_id=dev, device_id_type=MESH,
         )
-
-    lo, hi = pl.ds(0, CUT), pl.ds(CUT, PW - CUT)
 
     def out(k, j):
         if k == Z:
@@ -209,14 +217,8 @@
             return ring(sbuf.at[j], gbuf.at[j, b, a], k, j, dev_ar)
         if k == A_R:
             return ring(sbuf.at[j], gbuf.at[j, b, a], k, j, dev_al)
-        if k == F_L:
-            return ring(gbuf.at[j, b, a, :, lo], fst0.at[j], k, j, dev_ar)
-        if k == F_R:
-            return ring(gbuf.at[j, b, a, :, hi], fst1.at[j], k, j, dev_al)
-        if k == G_L:
-            return ring(fst0.at[j], gbuf.at[j, b, al, :, lo], k, j, dev_ar)
-        if k == G_R:
-            return ring(fst1.at[j], gbuf.at[j, b, ar, :, hi], k, j, dev_al)
+        if k == A_O:
+            return ring(gbuf.at[j, b, a], gbuf.at[j, b, a], k, j, dev_ao)
         if k == B_L:
             return ring(gbuf.at[j, b], gbuf.at[j, b], k, j, dev_br)
         if k == B_R:
@@ -239,54 +241,29 @@
             return ring(qbuf.at[j, b, ar], an.at[j, 0], k, j, dev_ar)
         if k == AN_R:
             return ring(qbuf.at[j, b, al], an.at[j, 1], k, j, dev_al)
-        if k == AO_L:
-            return ring(qbuf.at[j, b, aopp, :, lo], afs0.at[j], k, j, dev_ar)
-        if k == AO_R:
-            return ring(qbuf.at[j, b, aopp, :, hi], afs1.at[j], k, j, dev_al)
-        if k == AF_L:
-            return ring(afs0.at[j], ao.at[j, :, lo], k, j, dev_ar)
-        if k == AF_R:
-            return ring(afs1.at[j], ao.at[j, :, hi], k, j, dev_al)
+        if k == AN_O:
+            return ring(qbuf.at[j, b, aopp], ao.at[j], k, j, dev_ao)
         to = jnp.where(j < NC, nxt, prv)
         h = k - FIN0
         dev = {"section": to, "expert": exp if h == 0 else partner}
         return ring(fbuf.at[j, h], fin.at[j, h], k, j, dev)
 
-    def arrived(k, j):
-        dst = {
-            Z: lambda: zin.at[j],
-            A_L: lambda: gbuf.at[j, b, al],
-            A_R: lambda: gbuf.at[j, b, ar],
-            F_L: lambda: fst0.at[j],
-            F_R: lambda: fst1.at[j],
-            G_L: lambda: gbuf.at[j, b, aopp, :, lo],
-            G_R: lambda: gbuf.at[j, b, aopp, :, hi],
-            B_L: lambda: gbuf.at[j, bl],
-            B_R: lambda: gbuf.at[j, br],
-            FB_L: lambda: gbuf.at[j, bopp, pl.ds(0, 2)],
-            FB_R: lambda: gbuf.at[j, bopp, pl.ds(2, 2)],
-            BO_L: lambda: bo.at[j, 0],
-            BO_R: lambda: bo.at[j, 1],
-            BN_L: lambda: bn.at[j, 0],
-            BN_R: lambda: bn.at[j, 1],
-            AN_L: lambda: an.at[j, 0],
-            AN_R: lambda: an.at[j, 1],
-            AO_L: lambda: afs0.at[j],
-            AO_R: lambda: afs1.at[j],
-            AF_L: lambda: ao.at[j, :, lo],
-            AF_R: lambda: ao.at[j, :, hi],
-            FIN0: lambda: fin.at[j, 0],
-            FIN1: lambda: fin.at[j, 1],
-        }[k]()
-        ring(dst, dst, k, j, dev_z).wait_recv()
+    def sized(n, sends, recvs):
+        ref = size.at[pl.ds(0, n)]
+        return pltpu.make_async_remote_copy(
+            src_ref=ref, dst_ref=ref, send_sem=sends, recv_sem=recvs,
+            device_id=dev_z, device_id_type=MESH,
+        )
+
+    def arrived(g, j):
+        sized(BLOCKS[g], ssem.at[0, j], rsem.at[g, j]).wait_recv()
 
     def send(*kinds, j):
         for k in kinds:
             out(k, j).start()
 
-    def sent(*kinds, j):
-        for k in kinds:
-            out(k, j).wait_send()
+    def sent(part, j):
+        sized(SENT[part], ssem.at[part, j], rsem.at[0, j]).wait_send()
 
     def f32(v):
         return v.astype(F32)
@@ -489,41 +466,29 @@
 
         @event(E1)
         def _(j):
-            arrived(Z, j)
+            arrived(GZ, j)
             by_half(j)
-            send(A_L, A_R, F_L, F_R, j=j)
-
-            @pl.when(j < NC)
-            def _():
-                weight(W_G, j).start()
-                weight(W_U, j).start()
-
-            @pl.when(j >= NC)
-            def _():
-                weight(W_DL, j - NC).start()
-                weight(W_DR, j - NC).start()
+            send(A_L, A_R, A_O, j=j)
+
+            @pl.when(j + AHEAD < NC)
+            def _():
+                weight(W_G, j + AHEAD).start()
+                weight(W_U, j + AHEAD).start()
+
+            @pl.when((j + AHEAD >= NC) & (j + AHEAD < NJ))
+            def _():
+                weight(W_DL, j + AHEAD - NC).start()
+                weight(W_DR, j + AHEAD - NC).start()
 
         @event(E2)
         def _(j):
-            arrived(F_L, j)
-            send(G_L, j=j)
-            arrived(F_R, j)
-            send(G_R, j=j)
+            arrived(GA, j)
+            send(B_L, B_R, j=j)
 
         @event(E3)
         def _(j):
-            arrived(A_L, j)
-            arrived(A_R, j)
-            arrived(G_L, j)
-            arrived(G_R, j)
-            send(B_L, B_R, j=j)
-
-        @event(E4)
-        def _(j):
-            arrived(B_L, j)
-            send(FB_L, j=j)
-            arrived(B_R, j)
-            send(FB_R, j=j)
+            arrived(GB, j)
+            send(FB_L, FB_R, j=j)
 
         for step, act_now in ((X1, hidden_own), (X2, hidden_all), (X3, grads_own), (X4, grads_all)):
             pl.when(t == step)(act_now)
@@ -546,12 +511,10 @@
 
         @event(R1)
         def _(j):
-            arrived(BO_L, j)
+            arrived(GBO, j)
             qbuf[j, br, 0:2] = (f32(qbuf[j, br, 0:2]) + f32(bo[j, 0])).astype(BF)
-            send(BN_L, j=j)
-            arrived(BO_R, j)
             qbuf[j, bl, 2:4] = (f32(qbuf[j, bl, 2:4]) + f32(bo[j, 1])).astype(BF)
-            send(BN_R, j=j)
+            send(BN_L, BN_R, j=j)
 
             @pl.when(j == NC)
             def _():
@@ -562,10 +525,9 @@
 
         @event(R2)
         def _(j):
-            arrived(BN_L, j)
-            arrived(BN_R, j)
+            arrived(GBN, j)
             qbuf[j, b] = (f32(qbuf[j, b]) + f32(bn[j, 0]) + f32(bn[j, 1])).astype(BF)
-            send(AO_L, AO_R, AN_L, AN_R, j=j)
+            send(AN_L, AN_R, AN_O, j=j)
 
             @pl.when(j == NC)
             def _():
@@ -576,24 +538,7 @@
 
         @event(R3)
         def _(j):
-            arrived(AO_L, j)
-            send(AF_L, j=j)
-            arrived(AO_R, j)
-            send(AF_R, j=j)
-
-            @pl.when(j == NC)
-            def _():
-                extra(dbuf.at[b, aopp], dao, DAO, dev_ar).wait()
-                dbuf[b, ar] = dbuf[b, ar] + dao[...]
-                extra(dbuf.at[b, ar], dan.at[0], DAN_L, dev_ar).start()
-                extra(dbuf.at[b, al], dan.at[1], DAN_R, dev_al).start()
-
-        @event(R4)
-        def _(j):
-            arrived(AN_L, j)
-            arrived(AN_R, j)
-            arrived(AF_L, j)
-            arrived(AF_R, j)
+            arrived(GAN, j)
             mine = f32(qbuf[j, b, a]) + f32(ao[j])
             theirs = f32(an[j, 0]) + f32(an[j, 1])
             first = jnp.where(half == 0, mine, theirs)
@@ -605,15 +550,21 @@
 
             @pl.when(j == NC)
             def _():
+                extra(dbuf.at[b, aopp], dao, DAO, dev_ar).wait()
+                dbuf[b, ar] = dbuf[b, ar] + dao[...]
+                extra(dbuf.at[b, ar], dan.at[0], DAN_L, dev_ar).start()
+                extra(dbuf.at[b, al], dan.at[1], DAN_R, dev_al).start()
+
+        @event(R4)
+        def _(j):
+            @pl.when(j == NC)
+            def _():
                 extra(dbuf.at[b, ar], dan.at[0], DAN_L, dev_ar).wait()
                 extra(dbuf.at[b, al], dan.at[1], DAN_R, dev_al).wait()
                 dfin[...] = dbuf[b, a] + dan[0] + dan[1]
                 extra(dfin, dz, DZ, dev_z).start()
 
-        @event(R5)
-        def _(j):
-            arrived(FIN0, j)
-            arrived(FIN1, j)
+            arrived(GFIN, j)
             v = jnp.concatenate(
                 [fin[j, h, :, c * FFD:(c + 1) * FFD] for h in range(2) for c in range(5)], axis=0
             )
@@ -621,11 +572,9 @@
             for k in range(8):
                 ubuf[j, :, k * FFD:(k + 1) * FFD] = u[k * 32:(k + 1) * 32]
             pltpu.make_async_copy(ubuf.at[j], u_out.at[j], usem.at[j]).start()
-            sent(
-                BO_L, BO_R, BN_L, BN_R, AN_L, AN_R, AO_L, AO_R, AF_L, AF_R, FIN0, FIN1, j=j
-            )
-
-            @pl.when(j == NC)
+            sent(1, j)
+
+            @pl.when(j == NC + 2)
             def _():
                 extra(dfin, dz, DZ, dev_z).wait()
                 la = iota((8, FFD), 0)
@@ -644,14 +593,13 @@
                 ggb[...] = total
                 pltpu.make_async_copy(ggb, gg_out, osem).start()
 
-        @event(E5)
+        @event(E4)
         def _(j):
             @pl.when(j == 0)
             def _():
                 saved()
 
-            arrived(FB_L, j)
-            arrived(FB_R, j)
+            arrived(GFB, j)
             unpack(j)
 
             @pl.when(j < NC)
@@ -662,7 +610,7 @@
             def _():
                 backward_rows(j - NC)
 
-            sent(Z, A_L, A_R, F_L, F_R, G_L, G_R, B_L, B_R, FB_L, FB_R, j=j)
+            sent(0, j)
 
     for c in wt_copies:
         c.wait()
@@ -697,15 +645,11 @@
             vmem((NJ, SUB, PW), BF),
             vmem((NJ, SUB, PW), BF),
             vmem((NJ, 4, 4, SUB, PW), BF),
-            vmem((NJ, SUB, CUT), BF),
-            vmem((NJ, SUB, PW - CUT), BF),
             vmem((NJ, 4, 4, SUB, PW), BF),
             vmem((NJ, 2, 2, SUB, PW), BF),
             vmem((NJ, 2, 4, SUB, PW), BF),
             vmem((NJ, 2, SUB, PW), BF),
             vmem((NJ, SUB, PW), BF),
-            vmem((NJ, SUB, CUT), BF),
-            vmem((NJ, SUB, PW - CUT), BF),
             vmem((NJ, 2, SUB, PW), BF),
             vmem((NJ, 2, SUB, PW), BF),
             vmem((NJ, 32, CH), BF),
@@ -736,8 +680,9 @@
             vmem((8, FFD), F32),
             vmem((8, FFD), F32),
             vmem((8, TOK), F32),
-            dma((NK, NJ)),
-            dma((NK, NJ)),
+            vmem((SENT[1], SUB, PW), BF),
+            dma((2, NJ)),
+            dma((NG, NJ)),
             dma((4, NC)),
             dma((4, NC)),
             dma((NX,)),
@@ -754,44 +699,48 @@
     )(*args)
 
 
-def spread_kernel(uf, ub, wt, gg, next_ref, prev_ref, gg_ref, lhs):
-    @pl.when(pl.program_id(0) == 0)
-    def _():
-        gg_ref[0] = gg[...]
-        for p in range(2):
-            w = wt[p].T
-            hi = w.astype(BF)
-            lhs[p, :, 0:32] = hi
-            lhs[p, :, 32:64] = (w - hi.astype(F32)).astype(BF)
-
-    for p, (src, dst) in enumerate(((uf, next_ref), (ub, prev_ref))):
-        both = jnp.concatenate([src[0], src[0]], axis=0)
-        dst[0] = nn(lhs[p], both).astype(BF)
+def spread_kernel(u, wt, gg, next_ref, prev_ref, gg_ref, lhs, obuf, sems):
+    gg_ref[0] = gg[...]
+    for p in range(2):
+        w = wt[p].T
+        hi = w.astype(BF)
+        lhs[p, :, 0:32] = hi
+        lhs[p, :, 32:64] = (w - hi.astype(F32)).astype(BF)
+
+    def copy(j):
+        dst = next_ref if j < NC else prev_ref
+        return pltpu.make_async_copy(
+            obuf.at[j], dst.at[0, :, pl.ds((j % NC) * CH, CH)], sems.at[j]
+        )
+
+    for j in range(NJ):
+        both = jnp.concatenate([u[j], u[j]], axis=0)
+        obuf[j] = nn(lhs[j // NC], both).astype(BF)
+        copy(j).start()
+    for j in range(NJ):
+        copy(j).wait()
 
 
 def dense(u, wt, gg):
+    vmem = pl.BlockSpec(memory_space=pltpu.VMEM)
+    any_spec = pl.BlockSpec(memory_space=pl.ANY)
     return pl.pallas_call(
         spread_kernel,
-        grid=(NC,),
         out_shape=(
             jax.ShapeDtypeStruct((1, TOK, D), BF),
             jax.ShapeDtypeStruct((1, TOK, D), BF),
             jax.ShapeDtypeStruct((1, 8, TOK), F32),
         ),
-        in_specs=[
-            pl.BlockSpec((1, 32, CH), lambda i: (i, 0, 0)),
-            pl.BlockSpec((1, 32, CH), lambda i: (i + NC, 0, 0)),
-            pl.BlockSpec((2, 32, TOK), lambda i: (0, 0, 0)),
-            pl.BlockSpec((8, TOK), lambda i: (0, 0)),
+        in_specs=[vmem] * 3,
+        out_specs=(any_spec, any_spec, vmem),
+        scratch_shapes=[
+            pltpu.VMEM((2, TOK, 64), BF),
+            pltpu.VMEM((NJ, TOK, CH), BF),
+            pltpu.SemaphoreType.DMA((NJ,)),
         ],
-        out_specs=(
-            pl.BlockSpec((1, TOK, CH), lambda i: (0, 0, i)),
-            pl.BlockSpec((1, TOK, CH), lambda i: (0, 0, i)),
-            pl.BlockSpec((1, 8, TOK), lambda i: (0, 0, 0)),
-        ),
-        scratch_shapes=[pltpu.VMEM((2, TOK, 64), BF)],
+        compiler_params=pltpu.CompilerParams(vmem_limit_bytes=60 * 2**20),
         name="dense",
-    )(u, u, wt, gg)
+    )(u, wt, gg)
 
 
 def body(*args):

time: 121 us -> 106 us (0.88)
  Pallas kernels: 120 us -> 104 us
    pallas_call x1, Pallas kernels: 114 us -> 100 us  [relay(): pl.pallas_call(relay_kernel, out_shape=(jax.ShapeDtypeStruct((NJ, 32, CH)...]
    pallas_call x1, Pallas kernels: 5.96 us -> 4.09 us  [dense(): pl.pallas_call(spread_kernel, out_shape=(jax.ShapeDtypeStruct((1, TOK, D)...]
where the time goes in v4:
time: 106 us; the launch traced here: 105 us
  Pallas kernels  104 us (98%)
    pallas_call x1, Pallas kernels, relay(): pl.pallas_call(relay_kernel, out_shape=(jax.ShapeDtypeStruct((NJ, 32, CH)...  100 us
    pallas_call x1, Pallas kernels, dense(): pl.pallas_call(spread_kernel, out_shape=(jax.ShapeDtypeStruct((1, TOK, D)...  4.09 us

profile of v4, /device:TPU:1, one launch (start us, length us, event | category | flops | bytes accessed | tf_op | source)
XLA Modules:
  0.0 105.0 jit_solution(14255639794882036724)
XLA Ops:
  0.6 100.3 %relay.1 = (bf16[14,32,1024]{2,1,0:T(8,128)(2,1)}, f32[2,32,128]{2,1,0:T(8,128)}, f32[8,128]{1,0:T(8,128)}) custom-call(bf16[1,128,7168]{2,1,0:T(8,128)(2,1)} %act.1, bf16[1,128,7168]{2,1,0:T(8,128)(2,1)} %cot.1, s32[1,8,128]{2,1,0:T(8,128)} %bitcast.5, f32[1,8,128]{2,1,0:T(8,128)} %bitcast.6, s32[1,8,128]{2,1,0:T(8,128)} %bitcast.7, f32[1,8,128]{2,1,0:T(8,128)} %bitcast.8, ...), custom_call_target="tpu_custom_call" | custom-call | tf_op jit(solution)/shard_map/relay/pallas_call | solution.py:626
  100.9 4.1 %dense.1 = (bf16[1,128,7168]{2,1,0:T(8,128)(2,1)}, bf16[1,128,7168]{2,1,0:T(8,128)(2,1)}, f32[1,8,128]{2,1,0:T(8,128)}) custom-call(bf16[14,32,1024]{2,1,0:T(8,128)(2,1)} %get-tuple-element.9.u, f32[2,32,128]{2,1,0:T(8,128)} %get-tuple-element.10.wt, f32[8,128]{1,0:T(8,128)} %get-tuple-element.11.gg), custom_call_target="tpu_custom_call" | custom-call | tf_op jit(solution)/shard_map/dense/pallas_call | solution.py:727

commit v5 on v4

--- a/solution.py
+++ b/solution.py
@@ -455,6 +455,22 @@
                     f(t - lag)
             return wrap
 
+        @event(R0)
+        def _(j):
+            @pl.when(j < NC)
+            def _():
+                repack(j, nn(hcat[...], wd[j]))
+
+            @pl.when(j >= NC)
+            def _():
+                repack(j, nt(ggu[...], gu[j - NC]))
+
+            send(BO_L, BO_R, j=j)
+
+            @pl.when(j == NC)
+            def _():
+                extra(dbuf.at[bopp], dbo, DBO, dev_br).start()
+
         @event(0)
         def _(j):
             pack(j)
@@ -492,22 +508,6 @@
 
         for step, act_now in ((X1, hidden_own), (X2, hidden_all), (X3, grads_own), (X4, grads_all)):
             pl.when(t == step)(act_now)
-
-        @event(R0)
-        def _(j):
-            @pl.when(j < NC)
-            def _():
-                repack(j, nn(hcat[...], wd[j]))
-
-            @pl.when(j >= NC)
-            def _():
-                repack(j, nt(ggu[...], gu[j - NC]))
-
-            send(BO_L, BO_R, j=j)
-
-            @pl.when(j == NC)
-            def _():
-                extra(dbuf.at[bopp], dbo, DBO, dev_br).start()
 
         @event(R1)
         def _(j):

time: 106 us -> 104 us (0.981); the launches traced: 105 us -> 104 us
  no operation moved by 1% of the time
where the time goes in v5:
time: 104 us
  Pallas kernels  104 us (100%)
    pallas_call x1, Pallas kernels, relay(): pl.pallas_call(relay_kernel, out_shape=(jax.ShapeDtypeStruct((NJ, 32, CH)...  99.5 us
    pallas_call x1, Pallas kernels, dense(): pl.pallas_call(spread_kernel, out_shape=(jax.ShapeDtypeStruct((1, TOK, D)...  4.09 us

profile of v5, /device:TPU:1, one launch (start us, length us, event | category | flops | bytes accessed | tf_op | source)
XLA Modules:
  0.0 104.3 jit_solution(18323779451010407020)
XLA Ops:
  0.6 99.5 %relay.1 = (bf16[14,32,1024]{2,1,0:T(8,128)(2,1)}, f32[2,32,128]{2,1,0:T(8,128)}, f32[8,128]{1,0:T(8,128)}) custom-call(bf16[1,128,7168]{2,1,0:T(8,128)(2,1)} %act.1, bf16[1,128,7168]{2,1,0:T(8,128)(2,1)} %cot.1, s32[1,8,128]{2,1,0:T(8,128)} %bitcast.5, f32[1,8,128]{2,1,0:T(8,128)} %bitcast.6, s32[1,8,128]{2,1,0:T(8,128)} %bitcast.7, f32[1,8,128]{2,1,0:T(8,128)} %bitcast.8, ...), custom_call_target="tpu_custom_call" | custom-call | tf_op jit(solution)/shard_map/relay/pallas_call | solution.py:626
  100.2 4.1 %dense.1 = (bf16[1,128,7168]{2,1,0:T(8,128)(2,1)}, bf16[1,128,7168]{2,1,0:T(8,128)(2,1)}, f32[1,8,128]{2,1,0:T(8,128)}) custom-call(bf16[14,32,1024]{2,1,0:T(8,128)(2,1)} %get-tuple-element.9.u, f32[2,32,128]{2,1,0:T(8,128)} %get-tuple-element.10.wt, f32[8,128]{1,0:T(8,128)} %get-tuple-element.11.gg), custom_call_target="tpu_custom_call" | custom-call | tf_op jit(solution)/shard_map/dense/pallas_call | solution.py:727
